TPU v7x, 32 devices: a whole 2x2x4 slice. The times are simulated.
32 devices in a mesh: dp: 2 (over x), tp: 4 (over z), sp: 4 (over y, core).
Axes of the slice: x: 2, y: 2, z: 4, core: 2. Of those that a mesh axis runs over, the one named last changes fastest.
Arguments:
- tokens: bfloat16 [16, 3584], P('dp'), parts along dimension 0
- positions: int32 [16], P('dp'), parts along dimension 0
- cache_k: bfloat16 [16, 4096, 8, 256], P('dp', 'sp', 'tp'), parts along dimension 0
- cache_v: bfloat16 [16, 4096, 8, 256], P('dp', 'sp', 'tp'), parts along dimension 0
- attn_gain: bfloat16 [3584], replicated
- w_q: bfloat16 [3584, 4096], P(None, 'tp')
- w_k: bfloat16 [3584, 2048], P(None, 'tp')
- w_v: bfloat16 [3584, 2048], P(None, 'tp')
- w_o: bfloat16 [4096, 3584], P('tp')
- mlp_gain: bfloat16 [3584], replicated
- w_gate: bfloat16 [3584, 14336], P(None, 'tp')
- w_up: bfloat16 [3584, 14336], P(None, 'tp')
- w_down: bfloat16 [14336, 3584], P('tp')
Outputs:
- output 1: bfloat16 [16, 3584], P('dp'), parts along dimension 0
- output 2: bfloat16 [16, 4096, 8, 256], P('dp', 'sp', 'tp'), parts along dimension 0
- output 3: bfloat16 [16, 4096, 8, 256], P('dp', 'sp', 'tp'), parts along dimension 0
There are 2 independent parts. A program takes and returns all parts, laid end to end along the dimension named above; an argument that names none is the same for every part.
All inputs are finite; a program needn't handle non-finite values.
Results may differ from a plain program's by a relative error of at most 0.0088623.
Values sent between devices are 32-bit elements.
A program may use at most 1 GiB of HBM per device.

v0:
```python
import math
import jax
import jax.numpy as jnp
from jax import lax
from jax.sharding import PartitionSpec as P

NORM_EPS = 1e-5
ROPE_THETA = 10000.0


def rms_norm(values, gain):
    wide = values.astype(jnp.float32)
    inv_rms = lax.rsqrt(jnp.mean(wide * wide, axis=-1, keepdims=True) + NORM_EPS)
    return (wide * inv_rms * gain.astype(jnp.float32)).astype(jnp.bfloat16)


def rope_tables(positions, head_dim):
    frequencies = ROPE_THETA ** (-2.0 * jnp.arange(head_dim // 2, dtype=jnp.float32) / head_dim)
    angles = positions.astype(jnp.float32)[:, None] * frequencies[None, :]
    return jnp.cos(angles)[:, None, :], jnp.sin(angles)[:, None, :]


def apply_rope(vectors, cos_table, sin_table):
    half = vectors.shape[-1] // 2
    first = vectors[..., :half]
    second = vectors[..., half:]
    return jnp.concatenate([first * cos_table - second * sin_table, second * cos_table + first * sin_table], axis=-1)


def solution(mesh):
    sp_size = mesh.shape["sp"]
    cache_spec = P("dp", "sp", "tp", None)
    row_spec = P("dp", None)
    col_spec = P(None, "tp")
    in_specs = (row_spec, P("dp"), cache_spec, cache_spec, P(None), col_spec, col_spec, col_spec, P("tp", None), P(None), col_spec, col_spec, P("tp", None))
    out_specs = (row_spec, cache_spec, cache_spec)

    def local_step(tokens, positions, cache_k, cache_v, attn_gain, w_q, w_k, w_v, w_o, mlp_gain, w_gate, w_up, w_down):
        rows = tokens.shape[0]
        local_slots = cache_k.shape[1]
        kv_local = cache_k.shape[2]
        head_dim = cache_k.shape[3]
        heads_local = w_q.shape[1] // head_dim
        group = heads_local // kv_local
        slots = local_slots * sp_size
        slot_ids = lax.axis_index("sp") * local_slots + jnp.arange(local_slots)

        normed = rms_norm(tokens, attn_gain)
        cos_table, sin_table = rope_tables(positions, head_dim)
        q_lin = jnp.dot(normed, w_q, preferred_element_type=jnp.float32).reshape(rows, heads_local, head_dim)
        k_lin = jnp.dot(normed, w_k, preferred_element_type=jnp.float32).reshape(rows, kv_local, head_dim)
        v_new = jnp.dot(normed, w_v, preferred_element_type=jnp.float32).astype(jnp.bfloat16).reshape(rows, kv_local, head_dim)
        q_rot = apply_rope(q_lin, cos_table, sin_table).astype(jnp.bfloat16).reshape(rows, kv_local, group, head_dim)
        k_rot = apply_rope(k_lin, cos_table, sin_table).astype(jnp.bfloat16)

        hit_mask = (slot_ids[None, :] == (positions % slots)[:, None])[:, :, None, None]
        new_k = jnp.where(hit_mask, k_rot[:, None], cache_k)
        new_v = jnp.where(hit_mask, v_new[:, None], cache_v)

        scores = jnp.einsum("bkgd,bskd->bkgs", q_rot, new_k, preferred_element_type=jnp.float32) * (1.0 / math.sqrt(head_dim))
        valid = ((positions[:, None] >= slots - 1) | (slot_ids[None, :] <= positions[:, None]))[:, None, None, :]
        local_max = jnp.max(jnp.where(valid, scores, -jnp.inf), axis=-1)
        exp_scores = jnp.exp(jnp.where(valid, scores - local_max[..., None], -jnp.inf))
        local_sum = jnp.sum(exp_scores, axis=-1)
        local_out = jnp.einsum("bkgs,bskd->bkgd", exp_scores.astype(jnp.bfloat16), new_v, preferred_element_type=jnp.float32)

        global_max = lax.pmax(local_max, "sp")
        factor = jnp.exp(local_max - global_max)
        packed = jnp.concatenate([local_out * factor[..., None], (local_sum * factor)[..., None]], axis=-1)
        total = lax.psum(packed, "sp")
        attended = (total[..., :head_dim] / total[..., head_dim:]).astype(jnp.bfloat16).reshape(rows, heads_local * head_dim)

        attn_proj = lax.psum(jnp.dot(attended, w_o, preferred_element_type=jnp.float32), "tp")
        hidden = (tokens.astype(jnp.float32) + attn_proj).astype(jnp.bfloat16)
        normed_mlp = rms_norm(hidden, mlp_gain)
        gate_proj = jnp.dot(normed_mlp, w_gate, preferred_element_type=jnp.float32)
        up_proj = jnp.dot(normed_mlp, w_up, preferred_element_type=jnp.float32)
        activated = (jax.nn.silu(gate_proj) * up_proj).astype(jnp.bfloat16)
        mlp_down = lax.psum(jnp.dot(activated, w_down, preferred_element_type=jnp.float32), "tp")
        layer_out = (hidden.astype(jnp.float32) + mlp_down).astype(jnp.bfloat16)
        return layer_out, new_k, new_v

    return jax.shard_map(local_step, mesh=mesh, in_specs=in_specs, out_specs=out_specs, check_vma=False)
```

profile of v0, /device:TPU:0, one launch (start us, length us, event | category | flops | bytes accessed | tf_op | source)
XLA Modules:
  0.0 193.7 jit_solution(1905367929481578361)
XLA Ops:
  7.2 0.0 all-reduce.3.cloned.1.call-start
  7.2 0.7 broadcast_compare_fusion.1
  7.9 0.7 fusion.46
  8.6 1.0 fusion.12
  9.6 0.0 slice-start
  9.6 0.9 convert_element_type.49
  10.5 2.9 %convolution_convert_fusion = bf16[8,512]{1,0:T(8,128)(2,1)S(1)} fusion(bf16[3584,512]{1,0:T(8,128)(2,1)} %param.20, bf16[8,3584]{1,0:T(8,128)(2,1)} %param.13, f32[3584]{0:T(1024)S(1)} %convert_element_type.49, f32[8]{0:T(128)S(1)} %add_rsqrt_fusion.1), kind=kOutput, calls=%fused_computation.11 | convolution fusion | flops 29478912 | bytes 3749920 | tf_op jit(solution)/shard_map/dot_general | solution.py:52
  13.4 2.7 %fusion.41 = f32[8,512]{1,0:T(8,128)S(1)} fusion(bf16[3584,512]{1,0:T(8,128)(2,1)} %param.19, bf16[8,3584]{1,0:T(8,128)(2,1)} %param.13, f32[3584]{0:T(1024)S(1)} %convert_element_type.49, f32[8]{0:T(128)S(1)} %add_rsqrt_fusion.1), kind=kOutput, calls=%fused_computation.66 | convolution fusion | flops 29474816 | bytes 3758112 | tf_op jit(solution)/shard_map/dot_general | solution.py:51
  16.1 0.1 multiply_cosine_fusion
  16.2 0.0 slice-start.1
  16.3 4.4 %fusion.43 = f32[8,1024]{1,0:T(8,128)S(1)} fusion(bf16[3584,1024]{1,0:T(8,128)(2,1)} %param.18, bf16[8,3584]{1,0:T(8,128)(2,1)} %param.13, f32[3584]{0:T(1024)S(1)} %convert_element_type.49, f32[8]{0:T(128)S(1)} %add_rsqrt_fusion.1), kind=kOutput, calls=%fused_computation.67 | convolution fusion | flops 58834944 | bytes 7444512 | tf_op jit(solution)/shard_map/dot_general | solution.py:50
  20.7 0.1 compare_or_fusion
  20.8 28.5 %broadcast_select_fusion = (bf16[8,1024,2,256]{3,2,1,0:T(2,128)(2,1)}, bf16[8,1024,2,256]{3,2,1,0:T(2,128)(2,1)S(1)}) fusion(bf16[8,1024,2,256]{3,2,1,0:T(2,128)(2,1)S(1)} %bitcast.18, pred[8,1024]{1,0:T(8,128)(4,1)S(1)} %get-tuple-element.14, bf16[8,2,256]{2,1,0:T(2,128)(2,1)S(1)} %copy.31, bf16[8,1024,2,256]{3,2,1,0:T(2,128)(2,1)} %param.15, ...), kind=kLoop, calls=%fused_computation | loop fusion | flops 8388608 | bytes 33579008 | tf_op jit(solution)/shard_map/jit(_where)/select_n | solution.py:58
  49.3 3.4 %copy-done = bf16[8,1024,2,256]{3,2,1,0:T(2,128)(2,1)} copy-done((bf16[8,1024,2,256]{3,2,1,0:T(2,128)(2,1)}, bf16[8,1024,2,256]{3,2,1,0:T(2,128)(2,1)S(1)}, u32[]{:S(2)}) %copy-start) | copy-done | bytes 8388632
  52.7 2.4 %select_reduce_fusion = (f32[8,2,2]{2,1,0:T(2,128)S(1)}, f32[8,2,2,1024]{3,2,1,0:T(2,128)S(1)}) fusion(pred[8,1024]{1,0:T(8,128)(4,1)S(1)} %get-tuple-element.13, bf16[8,1024,2,256]{3,2,1,0:T(2,128)(2,1)S(1)} %get-tuple-element.12, bf16[8,2,2,128]{3,2,1,0:T(2,128)(2,1)S(1)} %bitcast.24, bf16[8,2,2,128]{3,2,1,0:T(2,128)(2,1)S(1)} %bitcast.23), kind=kOutput, calls=%fused_computation.19 | convolution fusion | flops 16908256 | bytes 8544384 | tf_op jit(solution)/shard_map/bkgd,bskd->bkgs/dot_general | solution.py:60
  55.1 8.6 %pmax.7 = f32[8,2,2]{2,1,0:T(2,128)S(1)} all-reduce(f32[8,2,2]{2,1,0:T(2,128)S(1)} %get-tuple-element.19), channel_id=1, replica_groups=mesh['dp'=2,'tp'=4,'sp'=4] {'sp'}, use_global_device_ids=true, to_apply=%region_2.3 | all-reduce | flops 32 | bytes 256 | tf_op jit(solution)/shard_map/pmax | solution.py:67
  63.6 0.3 fusion.28
  63.9 0.2 copy.34
  64.1 4.6 %fusion.9 = f32[8,2,2,256]{3,2,1,0:T(2,128)S(1)} fusion(bf16[8,1024,2,256]{3,2,1,0:T(2,128)(2,1)} %get-tuple-element.11, f32[8,2,2,1024]{3,2,1,0:T(2,128)S(1)} %get-tuple-element.20, pred[8,1024]{1,0:T(8,128)(4,1)S(1)} %get-tuple-element.13, f32[8,2,2]{2,1,0:T(2,128)S(1)} %get-tuple-element.19, f32[8,2,2]{2,1,0:T(2,128)S(1)} %get-tuple-element.6), kind=kOutput, calls=%fused_computation.10 | convolution fusion | flops 16883712 | bytes 8560896 | tf_op jit(solution)/shard_map/bkgs,bskd->bkgd/dot_general | solution.py:65
  68.8 10.6 %psum.21 = f32[8,2,2,257]{3,2,1,0:T(2,128)S(1)} all-reduce(f32[8,2,2,257]{3,2,1,0:T(2,128)S(1)} %pad_maximum_fusion), channel_id=1, replica_groups=mesh['dp'=2,'tp'=4,'sp'=4] {'sp'}, use_global_device_ids=true, to_apply=%region_4.5 | all-reduce | flops 8224 | bytes 65792 | tf_op jit(solution)/shard_map/psum | solution.py:70
  79.4 0.2 copy.39
  79.6 0.1 fusion.27
  79.7 4.8 %fusion.47 = f32[8,3584]{1,0:T(8,128)} fusion(bf16[8,1024]{1,0:T(8,128)(2,1)S(1)} %reshape.176, bf16[1024,3584]{1,0:T(8,128)(2,1)} %param.21), kind=kOutput, calls=%fused_computation.69 | convolution fusion | flops 58720256 | bytes 7471104 | tf_op jit(solution)/shard_map/dot_general | solution.py:73
  84.5 0.0 all-reduce.3.cloned.1.call-update
  84.5 0.0 all-reduce.5.cloned.1.call-start
  84.6 34.9 %all-reduce.3.cloned.1.call-done = f32[8,3584]{1,0:T(8,128)} async-done(((f32[8,3584]{1,0:T(8,128)}), f32[8,3584]{1,0:T(8,128)}) %all-reduce.3.cloned.1.call-update) | async-done | bytes 114704 | tf_op jit(solution)/shard_map/psum | solution.py:73
  119.5 1.0 fusion.16
  120.6 10.1 %fusion.34 = f32[8,3584]{1,0:T(8,128)S(1)} fusion(bf16[3584,3584]{1,0:T(8,128)(2,1)} %param.23, bf16[8,3584]{1,0:T(8,128)(2,1)S(1)} %get-tuple-element.4, f32[3584]{0:T(1024)S(1)} %convert_element_type.57, f32[8]{0:T(128)S(1)} %add_rsqrt_fusion), kind=kOutput, calls=%fused_computation.51 | convolution fusion | flops 205635584 | bytes 25876512 | tf_op jit(solution)/shard_map/dot_general | solution.py:76
  130.7 20.1 %fusion.5 = f32[8,3584]{1,0:T(8,128)} fusion(bf16[3584,3584]{1,0:T(8,128)(2,1)} %param.25, bf16[3584,3584]{1,0:T(8,128)(2,1)} %param.24, f32[8,3584]{1,0:T(8,128)S(1)} %fusion.34, bf16[8,3584]{1,0:T(8,128)(2,1)S(1)} %get-tuple-element.4, f32[3584]{0:T(1024)S(1)} %convert_element_type.57, f32[8]{0:T(128)S(1)} %add_rsqrt_fusion), kind=kOutput, calls=%fused_computation.8 | convolution fusion | flops 411328512 | bytes 51681312 | tf_op jit(solution)/shard_map/dot_general | solution.py:79
  150.8 0.0 all-reduce.5.cloned.1.call-update
  150.8 34.6 %all-reduce.5.cloned.1.call-done = f32[8,3584]{1,0:T(8,128)} async-done(((f32[8,3584]{1,0:T(8,128)}), f32[8,3584]{1,0:T(8,128)}) %all-reduce.5.cloned.1.call-update) | async-done | bytes 114704 | tf_op jit(solution)/shard_map/psum | solution.py:79
  185.4 1.5 fusion.19
  (26 shorter events, 0.2 us)
Async XLA Ops:
  7.2 13.5 %copy-start.3 = (s32[8]{0:T(128)S(1)}, s32[8]{0:T(128)}, u32[]{:S(2)}) copy-start(s32[8]{0:T(128)} %param.14) | copy-start | bytes 100
  7.2 112.3 %all-reduce.3.cloned.1.call-start = ((), (), s32[]{:S(2)}) async-start(), calls=%async_computation | async-start | bytes 229376 | tf_op jit(solution)/shard_map/psum | solution.py:73
  9.6 11.1 %slice-start = ((s8[8388608]{0:T(1024)(128)(4,1)}), s8[4194304]{0:T(1024)(128)(4,1)S(1)}, s32[]{:S(2)}) async-start(s8[8388608]{0:T(1024)(128)(4,1)} %bitcast.17), calls=%async_computation.2 | async-start | bytes 8388608
  16.2 4.6 %slice-start.1 = ((s8[8388608]{0:T(1024)(128)(4,1)}), s8[4194304]{0:T(1024)(128)(4,1)S(1)}, s32[]{:S(2)}) async-start(s8[8388608]{0:T(1024)(128)(4,1)} %bitcast.17), calls=%async_computation.3 | async-start | bytes 8388608
  49.3 3.4 %copy-start = (bf16[8,1024,2,256]{3,2,1,0:T(2,128)(2,1)}, bf16[8,1024,2,256]{3,2,1,0:T(2,128)(2,1)S(1)}, u32[]{:S(2)}) copy-start(bf16[8,1024,2,256]{3,2,1,0:T(2,128)(2,1)S(1)} %get-tuple-element.12) | copy-start | bytes 25165828
  68.8 15.8 %copy-start.2 = (bf16[3584]{0:T(1024)(128)(2,1)S(1)}, bf16[3584]{0:T(1024)(128)(2,1)}, u32[]{:S(2)}) copy-start(bf16[3584]{0:T(1024)(128)(2,1)} %param.22) | copy-start | bytes 21508
  68.8 50.7 %copy-start.1 = (bf16[8,3584]{1,0:T(8,128)(2,1)S(1)}, bf16[8,3584]{1,0:T(8,128)(2,1)}, u32[]{:S(2)}) copy-start(bf16[8,3584]{1,0:T(8,128)(2,1)} %param.13) | copy-start | bytes 172036
  84.5 100.8 %all-reduce.5.cloned.1.call-start = ((), (), s32[]{:S(2)}) async-start(), calls=%async_computation.1 | async-start | bytes 229376 | tf_op jit(solution)/shard_map/psum | solution.py:79
Sparse Core Ops, SparseCore 0:
  84.6 34.8 all-reduce.2
  150.9 34.3 all-reduce.4
where the time goes:
time: 194 us
  waiting for transfers between devices  69.5 us (36%)
  matrix products  51.9 us (27%)
  other arithmetic  35 us (18%)
  blocking collectives  19.1 us (10%)
  between operations  14.2 us (7%)
  local copies, waits for them, and re-layouts  3.89 us (2%)
    psum x1, waiting for transfers between devices, local_step(): lax.psum(jnp.dot(attended, w_o, preferred_element_type=jnp.float32), 'tp')  34.9 us
    psum x1, waiting for transfers between devices, local_step(): lax.psum(jnp.dot(activated, w_down, preferred_element_type=jnp.float32),...  34.6 us
    select_n x1, other arithmetic, local_step(): new_v = jnp.where(hit_mask, v_new[:, None], cache_v)  28.5 us
    dot_general x1, matrix products, local_step(): jnp.dot(activated, w_down, preferred_element_type=jnp.float32)  20.1 us
    psum x1, blocking collectives, local_step(): total = lax.psum(packed, 'sp')  10.6 us
    dot_general x1, matrix products, local_step(): gate_proj = jnp.dot(normed_mlp, w_gate, preferred_element_type=jnp.float32)  10.1 us
    pmax x1, blocking collectives, local_step(): global_max = lax.pmax(local_max, 'sp')  8.57 us
    dot_general x1, matrix products, local_step(): jnp.dot(attended, w_o, preferred_element_type=jnp.float32)  4.78 us
  transfers between devices with their start and end apart: 2, of which 2 were waited for; matrix products, arithmetic and copies ran while one was open for 0% of the time, Pallas kernels for 0%

commit v1 on v0

v1 whole, which is shorter than its diff:
```python
import math
import functools
import jax
import jax.numpy as jnp
from jax import lax
from jax.experimental import pallas as pl
from jax.experimental.pallas import tpu as pltpu
from jax.sharding import PartitionSpec as P

NORM_EPS = 1e-5
ROPE_THETA = 10000.0
MESH = pl.DeviceIdType.MESH
F32 = jnp.float32
BF16 = jnp.bfloat16


def rms_norm(wide, gain):
    inv_rms = lax.rsqrt(jnp.mean(wide * wide, axis=-1, keepdims=True) + NORM_EPS)
    return (wide * inv_rms * gain.astype(F32)).astype(BF16)


def rope_tables(positions, head_dim):
    frequencies = ROPE_THETA ** (-2.0 * jnp.arange(head_dim // 2, dtype=F32) / head_dim)
    angles = positions.astype(F32)[:, None] * frequencies[None, :]
    return jnp.cos(angles), jnp.sin(angles)


def attention_kernel(sp_size, chunks, pos_ref, tok_ref, gain_ref, cos_ref, sin_ref, wq, wk, wv, ck, cv,
                     new_k, new_v, packed_ref,
                     wbuf, kbuf, vbuf, q3, k3, v3, o3, m3, l3, wsem, ksem, vsem, okm, ovm):
    rows, local_slots, kv_local, head_dim = kbuf.shape
    slots = local_slots * sp_size
    depth = tok_ref.shape[1]
    q_width, kv_width = wq.shape[1], wk.shape[1]
    heads = q_width // head_dim
    group = heads // kv_local
    half = head_dim // 2
    step = depth // chunks
    first_slot = lax.axis_index("sp") * local_slots

    weight_copies = []
    for c in range(chunks):
        part = pl.ds(c * step, step)
        trio = [
            pltpu.make_async_copy(wq.at[part, :], wbuf.at[part, pl.ds(0, q_width)], wsem.at[c, 0]),
            pltpu.make_async_copy(wk.at[part, :], wbuf.at[part, pl.ds(q_width, kv_width)], wsem.at[c, 1]),
            pltpu.make_async_copy(wv.at[part, :], wbuf.at[part, pl.ds(q_width + kv_width, kv_width)], wsem.at[c, 2]),
        ]
        for copy in trio:
            copy.start()
        weight_copies.append(trio)
    k_in, v_in = [], []
    for b in range(rows):
        k_in.append(pltpu.make_async_copy(ck.at[b], kbuf.at[b], ksem.at[b]))
        v_in.append(pltpu.make_async_copy(cv.at[b], vbuf.at[b], vsem.at[b]))
        k_in[b].start()
        v_in[b].start()

    normed = rms_norm(tok_ref[...].astype(F32), gain_ref[...])
    acc = jnp.zeros((rows, q_width + 2 * kv_width), F32)
    for c in range(chunks):
        for copy in weight_copies[c]:
            copy.wait()
        acc = acc + jnp.dot(normed[:, c * step:(c + 1) * step], wbuf[c * step:(c + 1) * step, :], preferred_element_type=F32)

    cos_table, sin_table = cos_ref[...], sin_ref[...]
    scale = 1.0 / math.sqrt(head_dim)

    def rotate(start):
        a = acc[:, start:start + half]
        b = acc[:, start + half:start + head_dim]
        return a * cos_table - b * sin_table, b * cos_table + a * sin_table

    for j in range(heads):
        a, b = rotate(j * head_dim)
        q3[:, j, 0:half] = a
        q3[:, j, half:head_dim] = b
    for j in range(kv_local):
        a, b = rotate(q_width + j * head_dim)
        k3[:, j, 0:half] = a
        k3[:, j, half:head_dim] = b
        start = q_width + kv_width + j * head_dim
        v3[:, j, :] = acc[:, start:start + head_dim]

    width = local_slots * kv_local
    column = lax.broadcasted_iota(jnp.int32, (heads, width), 1)
    own_head = lax.rem(column, kv_local) == lax.broadcasted_iota(jnp.int32, (heads, width), 0) // group
    slot_ids = first_slot + column // kv_local
    k_out, v_out = [], []
    for b in range(rows):
        position = pos_ref[b]
        target = lax.rem(position, slots) - first_slot
        k_in[b].wait()
        v_in[b].wait()

        @pl.when((target >= 0) & (target < local_slots))
        def _():
            kbuf[b, target] = k3[b].astype(BF16)
            vbuf[b, target] = v3[b].astype(BF16)

        q_b = q3[b].astype(BF16)
        keys = kbuf[b].reshape(width, head_dim)
        scores = lax.dot_general(q_b, keys, (((1,), (1,)), ((), ())), preferred_element_type=F32) * scale
        limit = jnp.where(position >= slots - 1, slots, position)
        valid = own_head & (slot_ids <= limit)
        scores = jnp.where(valid, scores, -jnp.inf)
        top = jnp.max(scores, axis=1, keepdims=True)
        weights = jnp.where(valid, jnp.exp(scores - top), 0.0)
        k_out.append(pltpu.make_async_copy(kbuf.at[b], new_k.at[b], okm.at[b]))
        v_out.append(pltpu.make_async_copy(vbuf.at[b], new_v.at[b], ovm.at[b]))
        k_out[b].start()
        v_out[b].start()
        o3[b] = jnp.dot(weights.astype(BF16), vbuf[b].reshape(width, head_dim), preferred_element_type=F32)
        m3[b] = jnp.broadcast_to(top, (heads, 128))
        l3[b] = jnp.broadcast_to(jnp.sum(weights, axis=1, keepdims=True), (heads, 128))

    lane = lax.broadcasted_iota(jnp.int32, (rows, 128), 1) // 16
    stats = jnp.zeros((rows, 128), F32)
    for j in range(heads):
        packed_ref[:, j * head_dim:(j + 1) * head_dim] = o3[:, j, :]
        stats = jnp.where(lane == j, m3[:, j, :], stats)
        stats = jnp.where(lane == heads + j, l3[:, j, :], stats)
    packed_ref[:, q_width:q_width + 128] = stats
    for b in range(rows):
        k_out[b].wait()
        v_out[b].wait()


def exchange(axis, source, slots_ref, send_sem, recv_sem):
    me = lax.axis_index(axis)
    size = slots_ref.shape[0]
    copies = []
    for d in range(1, size):
        copy = pltpu.make_async_remote_copy(
            src_ref=source, dst_ref=slots_ref.at[me], send_sem=send_sem.at[d - 1], recv_sem=recv_sem.at[d - 1],
            device_id={axis: lax.rem(me + d, size)}, device_id_type=MESH)
        copy.start()
        copies.append(copy)
    return copies


def finish(copies):
    for copy in copies:
        copy.wait()


def mlp_kernel(head_dim, packed_ref, tok_ref, gain_ref, wo, wg, wu, wd, out_ref,
               wo_buf, wgu_buf, wd_buf, r1, part2, r2, part3, r3, part4, r4, part5, r5, part6, r6,
               wsem, ssem, rsem):
    rows, depth = tok_ref.shape
    sp_size, tp_size = r1.shape[0], r2.shape[0]
    q_width = wo.shape[0]
    heads = q_width // head_dim
    width = depth // sp_size
    hidden_width = wg.shape[1] // sp_size
    sp = lax.axis_index("sp")
    tp = lax.axis_index("tp")
    my_cols = pl.ds(pl.multiple_of(sp * width, 128), width)
    my_hidden = pl.ds(pl.multiple_of(sp * hidden_width, 128), hidden_width)

    barrier = pltpu.get_barrier_semaphore()
    for axis, me, size in (("sp", sp, sp_size), ("tp", tp, tp_size)):
        for d in range(1, size):
            pl.semaphore_signal(barrier, inc=1, device_id={axis: lax.rem(me + d, size)}, device_id_type=MESH)
    loads = [
        pltpu.make_async_copy(wo.at[:, my_cols], wo_buf, wsem.at[0]),
        pltpu.make_async_copy(wg.at[:, my_hidden], wgu_buf.at[:, pl.ds(0, hidden_width)], wsem.at[1]),
        pltpu.make_async_copy(wu.at[:, my_hidden], wgu_buf.at[:, pl.ds(hidden_width, hidden_width)], wsem.at[2]),
        pltpu.make_async_copy(wd.at[:, my_cols], wd_buf, wsem.at[3]),
    ]
    for copy in loads:
        copy.start()
    pl.semaphore_wait(barrier, sp_size + tp_size - 2)

    copies = exchange("sp", packed_ref, r1, ssem.at[0], rsem.at[0])
    r1[sp] = packed_ref[...]
    loads[0].wait()
    finish(copies)
    stats = [r1[s, :, q_width:q_width + 128] for s in range(sp_size)]
    pieces = []
    for j in range(heads):
        tops = [t[:, j * 16:j * 16 + 1] for t in stats]
        best = functools.reduce(jnp.maximum, tops)
        numerator = jnp.zeros((rows, head_dim), F32)
        denominator = jnp.zeros((rows, 1), F32)
        for s in range(sp_size):
            factor = jnp.exp(tops[s] - best)
            numerator = numerator + r1[s, :, j * head_dim:(j + 1) * head_dim] * factor
            denominator = denominator + stats[s][:, (heads + j) * 16:(heads + j) * 16 + 1] * factor
        pieces.append((numerator / denominator).astype(BF16))
    attended = jnp.concatenate(pieces, axis=1)
    part2[...] = jnp.dot(attended, wo_buf[...], preferred_element_type=F32)

    copies = exchange("tp", part2, r2, ssem.at[1], rsem.at[1])
    r2[tp] = part2[...]
    tokens_chunk = tok_ref[:, my_cols].astype(F32)
    finish(copies)
    total = r2[0]
    for t in range(1, tp_size):
        total = total + r2[t]
    hidden_chunk = (tokens_chunk + total).astype(BF16).astype(F32)
    part3[...] = hidden_chunk

    copies = exchange("sp", part3, r3, ssem.at[2], rsem.at[2])
    r3[sp] = hidden_chunk
    loads[1].wait()
    loads[2].wait()
    finish(copies)
    hidden = jnp.concatenate([r3[s] for s in range(sp_size)], axis=1)
    normed = rms_norm(hidden, gain_ref[...])
    both = jnp.dot(normed, wgu_buf[...], preferred_element_type=F32)
    gate, up = both[:, :hidden_width], both[:, hidden_width:]
    active = (gate * jax.nn.sigmoid(gate) * up).astype(BF16).astype(F32)
    part4[...] = active

    copies = exchange("sp", part4, r4, ssem.at[3], rsem.at[3])
    r4[sp] = active
    loads[3].wait()
    finish(copies)
    activated = jnp.concatenate([r4[s] for s in range(sp_size)], axis=1).astype(BF16)
    part5[...] = jnp.dot(activated, wd_buf[...], preferred_element_type=F32)

    copies = exchange("tp", part5, r5, ssem.at[4], rsem.at[4])
    r5[tp] = part5[...]
    finish(copies)
    total = r5[0]
    for t in range(1, tp_size):
        total = total + r5[t]
    out_chunk = (hidden_chunk + total).astype(BF16).astype(F32)
    part6[...] = out_chunk

    copies = exchange("sp", part6, r6, ssem.at[5], rsem.at[5])
    r6[sp] = out_chunk
    finish(copies)
    out_ref[...] = jnp.concatenate([r6[s] for s in range(sp_size)], axis=1).astype(BF16)


def solution(mesh):
    sp_size, tp_size = mesh.shape["sp"], mesh.shape["tp"]
    cache_spec = P("dp", "sp", "tp", None)
    row_spec = P("dp", None)
    col_spec = P(None, "tp")
    in_specs = (row_spec, P("dp"), cache_spec, cache_spec, P(None), col_spec, col_spec, col_spec, P("tp", None), P(None), col_spec, col_spec, P("tp", None))
    out_specs = (row_spec, cache_spec, cache_spec)

    def local_step(tokens, positions, cache_k, cache_v, attn_gain, w_q, w_k, w_v, w_o, mlp_gain, w_gate, w_up, w_down):
        rows, depth = tokens.shape
        head_dim = cache_k.shape[3]
        kv_local = cache_k.shape[2]
        q_width, kv_width = w_q.shape[1], w_k.shape[1]
        heads = q_width // head_dim
        width = depth // sp_size
        hidden_width = w_gate.shape[1] // sp_size
        chunks = 7
        cos_table, sin_table = rope_tables(positions, head_dim)
        vmem = pl.BlockSpec(memory_space=pltpu.VMEM)
        hbm = pl.BlockSpec(memory_space=pltpu.HBM)
        dma = pltpu.SemaphoreType.DMA
        in_hbm = functools.partial(pltpu.with_memory_space_constraint, memory_space=pltpu.HBM)
        new_k, new_v, packed = pl.pallas_call(
            functools.partial(attention_kernel, sp_size, chunks),
            out_shape=[pltpu.HBM(cache_k.shape, BF16), pltpu.HBM(cache_v.shape, BF16),
                       pltpu.VMEM((rows, q_width + 128), F32)],
            in_specs=[pl.BlockSpec(memory_space=pltpu.SMEM)] + [vmem] * 4 + [hbm] * 5,
            out_specs=[hbm, hbm, vmem],
            scratch_shapes=[
                pltpu.VMEM((depth, q_width + 2 * kv_width), BF16),
                pltpu.VMEM(cache_k.shape, BF16), pltpu.VMEM(cache_v.shape, BF16),
                pltpu.VMEM((rows, heads, head_dim), F32), pltpu.VMEM((rows, kv_local, head_dim), F32),
                pltpu.VMEM((rows, kv_local, head_dim), F32), pltpu.VMEM((rows, heads, head_dim), F32),
                pltpu.VMEM((rows, heads, 128), F32), pltpu.VMEM((rows, heads, 128), F32),
                dma((chunks, 3)), dma((rows,)), dma((rows,)), dma((rows,)), dma((rows,)),
            ],
            compiler_params=pltpu.CompilerParams(vmem_limit_bytes=40 * 2 ** 20),
            cost_estimate=pl.CostEstimate(flops=10 ** 9, bytes_accessed=48 * 10 ** 6, transcendentals=0),
            name="attention",
        )(positions, tokens, attn_gain[None, :], cos_table, sin_table, *map(in_hbm, (w_q, w_k, w_v, cache_k, cache_v)))

        chunk = pltpu.VMEM((rows, width), F32)
        act = pltpu.VMEM((rows, hidden_width), F32)
        out = pl.pallas_call(
            functools.partial(mlp_kernel, head_dim),
            out_shape=jax.ShapeDtypeStruct((rows, depth), BF16),
            in_specs=[vmem] * 3 + [hbm] * 4,
            out_specs=vmem,
            scratch_shapes=[
                pltpu.VMEM((q_width, width), BF16), pltpu.VMEM((depth, 2 * hidden_width), BF16),
                pltpu.VMEM((w_down.shape[0], width), BF16),
                pltpu.VMEM((sp_size, rows, q_width + 128), F32),
                chunk, pltpu.VMEM((tp_size, rows, width), F32),
                chunk, pltpu.VMEM((sp_size, rows, width), F32),
                act, pltpu.VMEM((sp_size, rows, hidden_width), F32),
                chunk, pltpu.VMEM((tp_size, rows, width), F32),
                chunk, pltpu.VMEM((sp_size, rows, width), F32),
                dma((4,)), dma((6, 3)), dma((6, 3)),
            ],
            compiler_params=pltpu.CompilerParams(vmem_limit_bytes=40 * 2 ** 20, collective_id=0, has_side_effects=True),
            cost_estimate=pl.CostEstimate(flops=10 ** 9, bytes_accessed=21 * 10 ** 6, transcendentals=0),
            name="mlp",
        )(packed, tokens, mlp_gain[None, :], *map(in_hbm, (w_o, w_gate, w_up, w_down)))
        return out, new_k, new_v

    return jax.shard_map(local_step, mesh=mesh, in_specs=in_specs, out_specs=out_specs, check_vma=False)
```

time: 194 us -> 54.3 us (0.28)
  waiting for transfers between devices: 69.5 us -> 0 us
  matrix products: 51.9 us -> 0 us
  Pallas kernels: 0 us -> 49 us
  other arithmetic: 35 us -> 0.78 us
  blocking collectives: 19.1 us -> 0 us
  between operations: 14.2 us -> 0.67 us
    psum x2 -> x0, waiting for transfers between devices: 69.5 us -> none  [the longest x1 34.9 us: local_step(): lax.psum(jnp.dot(attended, w_o, preferred_element_type=jnp.float32), 'tp')]
    dot_general x8 -> x0, matrix products: 51.9 us -> none  [the longest x1 20.1 us: local_step(): jnp.dot(activated, w_down, preferred_element_type=jnp.float32)]
    pallas_call x0 -> x2, Pallas kernels: none -> 49 us  [the longest x1 29.8 us: local_step(): pl.pallas_call(functools.partial(mlp_kernel, head_dim), out_shape=jax.Sha...]
    select_n x1 -> x0, other arithmetic: 28.5 us -> none  [local_step(): new_v = jnp.where(hit_mask, v_new[:, None], cache_v)]
    psum x1 -> x0, blocking collectives: 10.6 us -> none  [local_step(): total = lax.psum(packed, 'sp')]
    pmax x1 -> x0, blocking collectives: 8.57 us -> none  [local_step(): global_max = lax.pmax(local_max, 'sp')]
    convert_element_type x5 -> x1, other arithmetic: 3.22 us -> 0.66 us  [rope_tables(): angles = positions.astype(F32)[:, None] * frequencies[None, :]]
    reduce_sum x3 -> x0, other arithmetic: 2.28 us -> none  [the longest x2 2.01 us: rms_norm(): jnp.mean(wide * wide, axis=-1, keepdims=True) + NORM_EPS]
  transfers between devices with their start and end apart: 2 -> 0, of which waited for: 2 -> 0; matrix products, arithmetic and copies ran while one was open for 0% -> 0% of each run, Pallas kernels for 0% -> 0%
where the time goes in v1:
time: 54.3 us; the launch traced here: 54 us
  Pallas kernels  49 us (90%)
  local copies, waits for them, and re-layouts  3.52 us (6%)
  other arithmetic  0.78 us (1%)
  between operations  0.67 us (1%)
    pallas_call x1, Pallas kernels, local_step(): pl.pallas_call(functools.partial(mlp_kernel, head_dim), out_shape=jax.Sha...  29.8 us
    pallas_call x1, Pallas kernels, local_step(): pl.pallas_call(functools.partial(attention_kernel, sp_size, chunks), out_...  19.2 us
    unnamed x7, local copies, waits for them, and re-layouts  2.1 us

profile of v1, /device:TPU:0, one launch (start us, length us, event | category | flops | bytes accessed | tf_op | source)
XLA Modules:
  0.0 54.0 jit_solution(5032027112815121549)
XLA Ops:
  0.6 0.7 %convert_element_type.3 = f32[8]{0:T(128)S(1)} convert(s32[8]{0:T(128)} %pos_ref.1) | non-fusion elementwise | flops 8 | bytes 64 | tf_op jit(solution)/shard_map/convert_element_type | solution.py:24
  1.3 0.1 multiply_sine_fusion
  1.4 0.7 %broadcast_in_dim.8.gain_ref = bf16[1,3584]{1,0:T(2,128)(2,1)S(1)} reshape(bf16[3584]{0:T(1024)(128)(2,1)} %param.17) | data formatting | bytes 14336 | tf_op jit(solution)/shard_map/broadcast_in_dim | solution.py:277
  2.1 0.7 %broadcast_in_dim.9.gain_ref = bf16[1,3584]{1,0:T(2,128)(2,1)S(1)} reshape(bf16[3584]{0:T(1024)(128)(2,1)} %param.22) | data formatting | bytes 14336 | tf_op jit(solution)/shard_map/broadcast_in_dim | solution.py:300
  2.8 0.0 copy-start
  2.9 0.8 %copy-done = bf16[8,3584]{1,0:T(8,128)(2,1)S(1)} copy-done((bf16[8,3584]{1,0:T(8,128)(2,1)S(1)}, bf16[8,3584]{1,0:T(8,128)(2,1)}, u32[]{:S(2)}) %copy-start) | copy-done | bytes 57368
  3.7 0.0 copy-start.2
  3.7 0.7 %copy-done.2 = s32[8]{0:T(128)S(1)} copy-done((s32[8]{0:T(128)S(1)}, s32[8]{0:T(128)}, u32[]{:S(2)}) %copy-start.2) | copy-done | bytes 56
  4.3 0.0 copy-start.1
  4.3 19.2 %attention.1 = (bf16[8,1024,2,256]{3,2,1,0:T(2,128)(2,1)}, bf16[8,1024,2,256]{3,2,1,0:T(2,128)(2,1)}, f32[8,1152]{1,0:T(8,128)S(1)}) custom-call(s32[8]{0:T(128)S(1)} %copy-done.2, bf16[8,3584]{1,0:T(8,128)(2,1)S(1)} %copy-done, bf16[1,3584]{1,0:T(2,128)(2,1)S(1)} %broadcast_in_dim.8.gain_ref, f32[8,128]{1,0:T(8,128)S(1)} %get-tuple-element.10.cos_ref, ...), custom_call_target="tpu_custom_call" | custom-call | flops 1000000000 | bytes 48000000 | tf_op jit(solution)/shard_map/attention/pallas_call | solution.py:260
  23.5 0.0 copy-done.1
  23.5 29.8 %mlp.1 = bf16[8,3584]{1,0:T(8,128)(2,1)S(1)} custom-call(f32[8,1152]{1,0:T(8,128)S(1)} %get-tuple-element.6.packed_ref, bf16[8,3584]{1,0:T(8,128)(2,1)S(1)} %copy-done.1, bf16[1,3584]{1,0:T(2,128)(2,1)S(1)} %broadcast_in_dim.9.gain_ref, bf16[1024,3584]{1,0:T(8,128)(2,1)} %wo.1, bf16[3584,3584]{1,0:T(8,128)(2,1)} %wg.1, bf16[3584,3584]{1,0:T(8,128)(2,1)} %wu.1, ...), custom_call_target="tpu_custom_call" | custom-call | flops 1000000000 | bytes 21000000 | tf_op jit(solution)/shard_map/mlp/pallas_call | solution.py:281
  53.4 0.6 %copy.17 = bf16[8,3584]{1,0:T(8,128)(2,1)} copy(bf16[8,3584]{1,0:T(8,128)(2,1)S(1)} %mlp.1) | data formatting | bytes 114688
  (1 shorter events, 0.0 us)
Async XLA Ops:
  2.8 0.8 %copy-start = (bf16[8,3584]{1,0:T(8,128)(2,1)S(1)}, bf16[8,3584]{1,0:T(8,128)(2,1)}, u32[]{:S(2)}) copy-start(bf16[8,3584]{1,0:T(8,128)(2,1)} %tok_ref.3) | copy-start | bytes 172036
  3.7 0.7 %copy-start.2 = (s32[8]{0:T(128)S(1)}, s32[8]{0:T(128)}, u32[]{:S(2)}) copy-start(s32[8]{0:T(128)} %pos_ref.1) | copy-start | bytes 100
  4.3 19.2 %copy-start.1 = (bf16[8,3584]{1,0:T(8,128)(2,1)S(1)}, bf16[8,3584]{1,0:T(8,128)(2,1)}, u32[]{:S(2)}) copy-start(bf16[8,3584]{1,0:T(8,128)(2,1)} %tok_ref.3) | copy-start | bytes 172036

commit v2 on v1

v2 whole, which is shorter than its diff:
```python
import math
import functools
import jax
import jax.numpy as jnp
from jax import lax
from jax.experimental import pallas as pl
from jax.experimental.pallas import tpu as pltpu
from jax.sharding import PartitionSpec as P

NORM_EPS = 1e-5
ROPE_THETA = 10000.0
MESH = pl.DeviceIdType.MESH
F32 = jnp.float32
BF16 = jnp.bfloat16


def rope_tables(positions, half):
    index = lax.broadcasted_iota(jnp.int32, (positions.shape[0], half), 1).astype(F32)
    angles = positions * jnp.exp(index * (-math.log(ROPE_THETA) / half))
    turns = jnp.floor(angles * (2.0 / math.pi) + 0.5)
    rest = ((angles - turns * 1.5703125) - turns * 4.837512969970703125e-4) - turns * 7.54978995489188216e-8
    square = rest * rest
    sine = rest + rest * square * (-1.0 / 6 + square * (1.0 / 120 + square * (-1.0 / 5040 + square * (1.0 / 362880))))
    cosine = 1.0 + square * (-0.5 + square * (1.0 / 24 + square * (-1.0 / 720 + square * (1.0 / 40320 - square * (1.0 / 3628800)))))
    quadrant = turns.astype(jnp.int32) & 3
    swap = (quadrant & 1) == 1
    cos_value = jnp.where(swap, sine, cosine)
    sin_value = jnp.where(swap, cosine, sine)
    return (jnp.where((quadrant == 1) | (quadrant == 2), -cos_value, cos_value),
            jnp.where(quadrant >= 2, -sin_value, sin_value))


def scaled_norm(wide, gain_ref):
    inv_rms = lax.rsqrt(jnp.mean(wide * wide, axis=-1, keepdims=True) + NORM_EPS)
    gain = gain_ref[...].astype(F32)
    pieces = [(wide[:, i * 128:(i + 1) * 128] * inv_rms * gain[i:i + 1]).astype(BF16) for i in range(wide.shape[1] // 128)]
    return jnp.concatenate(pieces, axis=1)


def attention_kernel(sp_size, chunks, positions, tokens, gain, wq, wk, wv, ck, cv,
                     new_k, new_v, packed_ref,
                     pos_ref, tok_ref, gain_ref, wbuf, kbuf, vbuf, q3, k3, v3, o3, m3, l3,
                     psem, wsem, ksem, vsem, okm, ovm):
    rows, local_slots, kv_local, head_dim = kbuf.shape
    slots = local_slots * sp_size
    depth = tok_ref.shape[1]
    q_width, kv_width = wq.shape[1], wk.shape[1]
    heads = q_width // head_dim
    group = heads // kv_local
    half = head_dim // 2
    step = depth // chunks
    first_slot = lax.axis_index("sp") * local_slots

    small = [pltpu.make_async_copy(tokens, tok_ref, psem.at[0]), pltpu.make_async_copy(gain, gain_ref, psem.at[1]),
             pltpu.make_async_copy(positions, pos_ref, psem.at[2])]
    for copy in small:
        copy.start()
    weight_copies = []
    for c in range(chunks):
        part = pl.ds(c * step, step)
        trio = [
            pltpu.make_async_copy(wq.at[part, :], wbuf.at[part, pl.ds(0, q_width)], wsem.at[c, 0]),
            pltpu.make_async_copy(wk.at[part, :], wbuf.at[part, pl.ds(q_width, kv_width)], wsem.at[c, 1]),
            pltpu.make_async_copy(wv.at[part, :], wbuf.at[part, pl.ds(q_width + kv_width, kv_width)], wsem.at[c, 2]),
        ]
        for copy in trio:
            copy.start()
        weight_copies.append(trio)
    k_in = [pltpu.make_async_copy(ck.at[b], kbuf.at[b], ksem.at[b]) for b in range(rows)]
    v_in = [pltpu.make_async_copy(cv.at[b], vbuf.at[b], vsem.at[b]) for b in range(rows)]
    started = 0

    for copy in small:
        copy.wait()
    normed = scaled_norm(tok_ref[...].astype(F32), gain_ref)
    acc = jnp.zeros((rows, q_width + 2 * kv_width), F32)
    for c in range(chunks):
        for copy in weight_copies[c]:
            copy.wait()
        while started < min(rows, (c + 1) * rows // chunks + 1):
            k_in[started].start()
            v_in[started].start()
            started += 1
        acc = acc + jnp.dot(normed[:, c * step:(c + 1) * step], wbuf[c * step:(c + 1) * step, :], preferred_element_type=F32)

    row = lax.broadcasted_iota(jnp.int32, (rows, half), 0)
    position_rows = jnp.zeros((rows, half), F32)
    for b in range(rows):
        position_rows = jnp.where(row == b, pos_ref[b].astype(F32), position_rows)
    cos_table, sin_table = rope_tables(position_rows, half)
    scale = 1.0 / math.sqrt(head_dim)

    def rotate(start):
        a = acc[:, start:start + half]
        b = acc[:, start + half:start + head_dim]
        return a * cos_table - b * sin_table, b * cos_table + a * sin_table

    for j in range(heads):
        a, b = rotate(j * head_dim)
        q3[:, j, 0:half] = a
        q3[:, j, half:head_dim] = b
    for j in range(kv_local):
        a, b = rotate(q_width + j * head_dim)
        k3[:, j, 0:half] = a
        k3[:, j, half:head_dim] = b
        start = q_width + kv_width + j * head_dim
        v3[:, j, :] = acc[:, start:start + head_dim]

    width = local_slots * kv_local
    column = lax.broadcasted_iota(jnp.int32, (heads, width), 1)
    own_head = lax.rem(column, kv_local) == lax.broadcasted_iota(jnp.int32, (heads, width), 0) // group
    slot_ids = first_slot + column // kv_local
    k_out, v_out = [], []
    for b in range(rows):
        position = pos_ref[b]
        target = lax.rem(position, slots) - first_slot
        k_in[b].wait()
        v_in[b].wait()

        @pl.when((target >= 0) & (target < local_slots))
        def _():
            kbuf[b, target] = k3[b].astype(BF16)
            vbuf[b, target] = v3[b].astype(BF16)

        q_b = q3[b].astype(BF16)
        keys = kbuf[b].reshape(width, head_dim)
        scores = lax.dot_general(q_b, keys, (((1,), (1,)), ((), ())), preferred_element_type=F32) * scale
        limit = jnp.where(position >= slots - 1, slots, position)
        valid = own_head & (slot_ids <= limit)
        scores = jnp.where(valid, scores, -jnp.inf)
        top = jnp.max(scores, axis=1, keepdims=True)
        weights = jnp.where(valid, jnp.exp(scores - top), 0.0)
        k_out.append(pltpu.make_async_copy(kbuf.at[b], new_k.at[b], okm.at[b]))
        v_out.append(pltpu.make_async_copy(vbuf.at[b], new_v.at[b], ovm.at[b]))
        k_out[b].start()
        v_out[b].start()
        o3[b] = jnp.dot(weights.astype(BF16), vbuf[b].reshape(width, head_dim), preferred_element_type=F32)
        m3[b] = jnp.broadcast_to(top, (heads, 128))
        l3[b] = jnp.broadcast_to(jnp.sum(weights, axis=1, keepdims=True), (heads, 128))

    lane = lax.broadcasted_iota(jnp.int32, (rows, 128), 1) // 16
    stats = jnp.zeros((rows, 128), F32)
    for j in range(heads):
        packed_ref[:, j * head_dim:(j + 1) * head_dim] = o3[:, j, :]
        stats = jnp.where(lane == j, m3[:, j, :], stats)
        stats = jnp.where(lane == heads + j, l3[:, j, :], stats)
    packed_ref[:, q_width:q_width + 128] = stats
    for b in range(rows):
        k_out[b].wait()
        v_out[b].wait()


def exchange(axis, source, slots_ref, cols, send_sem, recv_sem):
    me = lax.axis_index(axis)
    size = slots_ref.shape[0]
    copies = []
    for d in range(1, size):
        copy = pltpu.make_async_remote_copy(
            src_ref=source.at[:, cols], dst_ref=slots_ref.at[me, :, cols], send_sem=send_sem.at[d - 1],
            recv_sem=recv_sem.at[d - 1], device_id={axis: lax.rem(me + d, size)}, device_id_type=MESH)
        copy.start()
        copies.append(copy)
    return copies


def finish(copies):
    for copy in copies:
        copy.wait()


def added(slots_ref, cols):
    total = slots_ref[0, :, cols]
    for t in range(1, slots_ref.shape[0]):
        total = total + slots_ref[t, :, cols]
    return total


def mlp_kernel(head_dim, cuts, packed_ref, tokens, gain, wo, wg, wu, wd, out_ref,
               tok_ref, gain_ref, wo_buf, wgu_buf, wd_buf, r1, part2, r2, part3, r3, part4, r4, part5, r5, part6, r6,
               psem, wsem, gsem, dsem, ssem, rsem):
    rows, depth = tokens.shape
    sp_size, tp_size = r1.shape[0], r2.shape[0]
    q_width = wo.shape[0]
    heads = q_width // head_dim
    width = depth // sp_size
    sp = lax.axis_index("sp")
    tp = lax.axis_index("tp")
    start = pl.multiple_of(sp * width, 128)
    my_cols = pl.ds(start, width)
    pieces = [pl.ds(a, b - a) for a, b in zip((0,) + cuts[:-1], cuts)]

    barrier = pltpu.get_barrier_semaphore()
    for axis, me, size in (("sp", sp, sp_size), ("tp", tp, tp_size)):
        for d in range(1, size):
            pl.semaphore_signal(barrier, inc=1, device_id={axis: lax.rem(me + d, size)}, device_id_type=MESH)
    small = [pltpu.make_async_copy(tokens.at[:, my_cols], tok_ref, psem.at[0]), pltpu.make_async_copy(gain, gain_ref, psem.at[1])]
    o_load = pltpu.make_async_copy(wo.at[:, my_cols], wo_buf, wsem)
    gate_loads, down_loads = [], []
    for i, piece in enumerate(pieces):
        cols = pl.ds(start + piece.start, piece.size)
        gate_loads.append([
            pltpu.make_async_copy(wg.at[:, cols], wgu_buf.at[:, pl.ds(2 * piece.start, piece.size)], gsem.at[i, 0]),
            pltpu.make_async_copy(wu.at[:, cols], wgu_buf.at[:, pl.ds(2 * piece.start + piece.size, piece.size)], gsem.at[i, 1])])
        down_loads.append([
            pltpu.make_async_copy(wd.at[pl.ds(s * width + piece.start, piece.size), my_cols],
                                  wd_buf.at[pl.ds(sp_size * piece.start + s * piece.size, piece.size), :], dsem.at[i, s])
            for s in range(sp_size)])
    o_load.start()
    for copy in small:
        copy.start()
    for loads in gate_loads:
        for copy in loads:
            copy.start()
    pl.semaphore_wait(barrier, sp_size + tp_size - 2)

    copies = exchange("sp", packed_ref, r1, pl.ds(0, packed_ref.shape[1]), ssem.at[0, 0], rsem.at[0, 0])
    r1[sp] = packed_ref[...]
    o_load.wait()
    finish(copies)
    for loads in down_loads:
        for copy in loads:
            copy.start()
    stats = [r1[s, :, q_width:q_width + 128] for s in range(sp_size)]
    parts = []
    for j in range(heads):
        tops = [t[:, j * 16:j * 16 + 1] for t in stats]
        best = functools.reduce(jnp.maximum, tops)
        numerator = jnp.zeros((rows, head_dim), F32)
        denominator = jnp.zeros((rows, 1), F32)
        for s in range(sp_size):
            factor = jnp.exp(tops[s] - best)
            numerator = numerator + r1[s, :, j * head_dim:(j + 1) * head_dim] * factor
            denominator = denominator + stats[s][:, (heads + j) * 16:(heads + j) * 16 + 1] * factor
        parts.append((numerator / denominator).astype(BF16))
    attended = jnp.concatenate(parts, axis=1)

    def project(left, weights, source, slots_ref, phase):
        sent = []
        for i, piece in enumerate(pieces):
            source[:, piece] = sum(jnp.dot(l, w[:, piece], preferred_element_type=F32) for l, w in zip(left, weights))
            sent.append(exchange("tp", source, slots_ref, piece, ssem.at[phase, i], rsem.at[phase, i]))
            slots_ref[tp, :, piece] = source[:, piece]
        return sent

    def settle(base, sent, slots_ref, target, target_slots, phase):
        passed = []
        for i, piece in enumerate(pieces):
            finish(sent[i])
            value = (base[:, piece] + added(slots_ref, piece)).astype(BF16).astype(F32)
            target[:, piece] = value
            passed.append(exchange("sp", target, target_slots, piece, ssem.at[phase, i], rsem.at[phase, i]))
            target_slots[sp, :, piece] = value
        return passed

    sent = project([attended], [wo_buf], part2, r2, 1)
    finish(small)
    tok32 = tok_ref[...].astype(F32)
    part6[...] = tok32
    passed = settle(part6, sent, r2, part3, r3, 2)
    for loads in gate_loads:
        finish(loads)
    for copies in passed:
        finish(copies)
    hidden = jnp.concatenate([r3[s] for s in range(sp_size)], axis=1)
    normed = scaled_norm(hidden, gain_ref)

    moved = []
    for i, piece in enumerate(pieces):
        both = jnp.dot(normed, wgu_buf[:, 2 * piece.start:2 * (piece.start + piece.size)], preferred_element_type=F32)
        gate, up = both[:, :piece.size], both[:, piece.size:]
        active = (gate * jax.nn.sigmoid(gate) * up).astype(BF16).astype(F32)
        part4[:, piece] = active
        moved.append(exchange("sp", part4, r4, piece, ssem.at[3, i], rsem.at[3, i]))
        r4[sp, :, piece] = active
    left, weights = [], []
    for i, piece in enumerate(pieces):
        finish(down_loads[i])
    total = None
    for i, piece in enumerate(pieces):
        finish(moved[i])
        left = jnp.concatenate([r4[s, :, piece] for s in range(sp_size)], axis=1).astype(BF16)
        rows_of = wd_buf[sp_size * piece.start:sp_size * (piece.start + piece.size), :]
        if i + 1 < len(pieces):
            product = jnp.dot(left, rows_of, preferred_element_type=F32)
            total = product if total is None else total + product
    part5[...] = total
    sent = []
    for i, piece in enumerate(pieces):
        part5[:, piece] = part5[:, piece] + jnp.dot(left, rows_of[:, piece.start:piece.start + piece.size], preferred_element_type=F32)
        sent.append(exchange("tp", part5, r5, piece, ssem.at[4, i], rsem.at[4, i]))
        r5[tp, :, piece] = part5[:, piece]
    passed = settle(part3, sent, r5, part6, r6, 5)
    for copies in passed:
        finish(copies)
    out_ref[...] = jnp.concatenate([r6[s] for s in range(sp_size)], axis=1).astype(BF16)


def solution(mesh):
    sp_size, tp_size = mesh.shape["sp"], mesh.shape["tp"]
    cache_spec = P("dp", "sp", "tp", None)
    row_spec = P("dp", None)
    col_spec = P(None, "tp")
    in_specs = (row_spec, P("dp"), cache_spec, cache_spec, P(None), col_spec, col_spec, col_spec, P("tp", None), P(None), col_spec, col_spec, P("tp", None))
    out_specs = (row_spec, cache_spec, cache_spec)

    def local_step(tokens, positions, cache_k, cache_v, attn_gain, w_q, w_k, w_v, w_o, mlp_gain, w_gate, w_up, w_down):
        rows, depth = tokens.shape
        head_dim = cache_k.shape[3]
        kv_local = cache_k.shape[2]
        q_width, kv_width = w_q.shape[1], w_k.shape[1]
        heads = q_width // head_dim
        width = depth // sp_size
        hidden_width = w_gate.shape[1] // sp_size
        chunks = 7
        cuts = (512, width)
        vmem = pl.BlockSpec(memory_space=pltpu.VMEM)
        hbm = pl.BlockSpec(memory_space=pltpu.HBM)
        dma = pltpu.SemaphoreType.DMA
        in_hbm = functools.partial(pltpu.with_memory_space_constraint, memory_space=pltpu.HBM)
        new_k, new_v, packed = pl.pallas_call(
            functools.partial(attention_kernel, sp_size, chunks),
            out_shape=[pltpu.HBM(cache_k.shape, BF16), pltpu.HBM(cache_v.shape, BF16),
                       pltpu.VMEM((rows, q_width + 128), F32)],
            in_specs=[hbm] * 8,
            out_specs=[hbm, hbm, vmem],
            scratch_shapes=[
                pltpu.SMEM((rows,), jnp.int32), pltpu.VMEM((rows, depth), BF16), pltpu.VMEM((depth // 128, 128), BF16),
                pltpu.VMEM((depth, q_width + 2 * kv_width), BF16),
                pltpu.VMEM(cache_k.shape, BF16), pltpu.VMEM(cache_v.shape, BF16),
                pltpu.VMEM((rows, heads, head_dim), F32), pltpu.VMEM((rows, kv_local, head_dim), F32),
                pltpu.VMEM((rows, kv_local, head_dim), F32), pltpu.VMEM((rows, heads, head_dim), F32),
                pltpu.VMEM((rows, heads, 128), F32), pltpu.VMEM((rows, heads, 128), F32),
                dma((3,)), dma((chunks, 3)), dma((rows,)), dma((rows,)), dma((rows,)), dma((rows,)),
            ],
            compiler_params=pltpu.CompilerParams(vmem_limit_bytes=40 * 2 ** 20),
            cost_estimate=pl.CostEstimate(flops=10 ** 9, bytes_accessed=48 * 10 ** 6, transcendentals=0),
            name="attention",
        )(*map(in_hbm, (positions, tokens, attn_gain.reshape(depth // 128, 128), w_q, w_k, w_v, cache_k, cache_v)))

        chunk = pltpu.VMEM((rows, width), F32)
        act = pltpu.VMEM((rows, hidden_width), F32)
        out = pl.pallas_call(
            functools.partial(mlp_kernel, head_dim, cuts),
            out_shape=jax.ShapeDtypeStruct((rows, depth), BF16),
            in_specs=[vmem] + [hbm] * 6,
            out_specs=vmem,
            scratch_shapes=[
                pltpu.VMEM((rows, width), BF16), pltpu.VMEM((depth // 128, 128), BF16),
                pltpu.VMEM((q_width, width), BF16), pltpu.VMEM((depth, 2 * hidden_width), BF16),
                pltpu.VMEM((w_down.shape[0], width), BF16),
                pltpu.VMEM((sp_size, rows, q_width + 128), F32),
                chunk, pltpu.VMEM((tp_size, rows, width), F32),
                chunk, pltpu.VMEM((sp_size, rows, width), F32),
                act, pltpu.VMEM((sp_size, rows, hidden_width), F32),
                chunk, pltpu.VMEM((tp_size, rows, width), F32),
                chunk, pltpu.VMEM((sp_size, rows, width), F32),
                dma((2,)), dma, dma((len(cuts), 2)), dma((len(cuts), sp_size)),
                dma((6, len(cuts), 3)), dma((6, len(cuts), 3)),
            ],
            compiler_params=pltpu.CompilerParams(vmem_limit_bytes=40 * 2 ** 20, collective_id=0, has_side_effects=True),
            cost_estimate=pl.CostEstimate(flops=10 ** 9, bytes_accessed=21 * 10 ** 6, transcendentals=0),
            name="mlp",
        )(packed, *map(in_hbm, (tokens, mlp_gain.reshape(depth // 128, 128), w_o, w_gate, w_up, w_down)))
        return out, new_k, new_v

    return jax.shard_map(local_step, mesh=mesh, in_specs=in_specs, out_specs=out_specs, check_vma=False)
```

time: 54.3 us -> 47.9 us (0.88)
  local copies, waits for them, and re-layouts: 3.52 us -> 0.63 us
  Pallas kernels: 49 us -> 46.5 us
  other arithmetic: 0.78 us -> 0 us
    pallas_call x1, Pallas kernels: 19.2 us -> 17.1 us  [local_step(): pl.pallas_call(functools.partial(attention_kernel, sp_size, chunks), out_...]
    unnamed x7 -> x1, local copies, waits for them, and re-layouts: 2.1 us -> 0.63 us
    broadcast_in_dim x2 -> x0, local copies, waits for them, and re-layouts: 1.42 us -> none  [the longest x1 0.71 us: local_step(): attn_gain[None, :]]
    convert_element_type x1 -> x0, other arithmetic: 0.66 us -> none  [rope_tables(): angles = positions.astype(F32)[:, None] * frequencies[None, :]]
where the time goes in v2:
time: 47.9 us; the launch traced here: 47.8 us
  Pallas kernels  46.5 us (97%)
  between operations  0.65 us (1%)
  local copies, waits for them, and re-layouts  0.63 us (1%)
    pallas_call x1, Pallas kernels, local_step(): pl.pallas_call(functools.partial(mlp_kernel, head_dim, cuts), out_shape=j...  29.4 us
    pallas_call x1, Pallas kernels, local_step(): pl.pallas_call(functools.partial(attention_kernel, sp_size, chunks), out_...  17.1 us

profile of v2, /device:TPU:0, one launch (start us, length us, event | category | flops | bytes accessed | tf_op | source)
XLA Modules:
  0.0 47.8 jit_solution(18048149010305071301)
XLA Ops:
  0.6 17.1 %attention.1 = (bf16[8,1024,2,256]{3,2,1,0:T(2,128)(2,1)}, bf16[8,1024,2,256]{3,2,1,0:T(2,128)(2,1)}, f32[8,1152]{1,0:T(8,128)S(1)}) custom-call(s32[8]{0:T(128)} %positions.1, bf16[8,3584]{1,0:T(8,128)(2,1)} %tokens.3, bf16[28,128]{1,0:T(8,128)(2,1)} %bitcast.2, bf16[3584,1024]{1,0:T(8,128)(2,1)} %wq.1, bf16[3584,512]{1,0:T(8,128)(2,1)} %wk.1, ...), custom_call_target="tpu_custom_call" | custom-call | flops 1000000000 | bytes 48000000 | tf_op jit(solution)/shard_map/attention/pallas_call | solution.py:320
  17.7 29.4 %mlp.1 = bf16[8,3584]{1,0:T(8,128)(2,1)S(1)} custom-call(f32[8,1152]{1,0:T(8,128)S(1)} %get-tuple-element.6.packed_ref, bf16[8,3584]{1,0:T(8,128)(2,1)} %tokens.3, bf16[28,128]{1,0:T(8,128)(2,1)} %bitcast.3, bf16[1024,3584]{1,0:T(8,128)(2,1)} %wo.1, bf16[3584,3584]{1,0:T(8,128)(2,1)} %wg.1, bf16[3584,3584]{1,0:T(8,128)(2,1)} %wu.1, bf16[3584,3584]{1,0:T(8,128)(2,1)} %wd.1), custom_call_target="tpu_custom_call" | custom-call | flops 1000000000 | bytes 21000000 | tf_op jit(solution)/shard_map/mlp/pallas_call | solution.py:342
  47.1 0.6 %copy.17 = bf16[8,3584]{1,0:T(8,128)(2,1)} copy(bf16[8,3584]{1,0:T(8,128)(2,1)S(1)} %mlp.1) | data formatting | bytes 114688

commit v3 on v2

--- a/solution.py
+++ b/solution.py
@@ -38,9 +38,9 @@
 
 
 def attention_kernel(sp_size, chunks, positions, tokens, gain, wq, wk, wv, ck, cv,
-                     new_k, new_v, packed_ref,
-                     pos_ref, tok_ref, gain_ref, wbuf, kbuf, vbuf, q3, k3, v3, o3, m3, l3,
-                     psem, wsem, ksem, vsem, okm, ovm):
+                     kbuf, vbuf, packed_ref,
+                     pos_ref, tok_ref, gain_ref, wbuf, q3, k3, v3, o3, m3, l3,
+                     psem, wsem, ksem, vsem):
     rows, local_slots, kv_local, head_dim = kbuf.shape
     slots = local_slots * sp_size
     depth = tok_ref.shape[1]
@@ -110,7 +110,6 @@
     column = lax.broadcasted_iota(jnp.int32, (heads, width), 1)
     own_head = lax.rem(column, kv_local) == lax.broadcasted_iota(jnp.int32, (heads, width), 0) // group
     slot_ids = first_slot + column // kv_local
-    k_out, v_out = [], []
     for b in range(rows):
         position = pos_ref[b]
         target = lax.rem(position, slots) - first_slot
@@ -130,10 +129,6 @@
         scores = jnp.where(valid, scores, -jnp.inf)
         top = jnp.max(scores, axis=1, keepdims=True)
         weights = jnp.where(valid, jnp.exp(scores - top), 0.0)
-        k_out.append(pltpu.make_async_copy(kbuf.at[b], new_k.at[b], okm.at[b]))
-        v_out.append(pltpu.make_async_copy(vbuf.at[b], new_v.at[b], ovm.at[b]))
-        k_out[b].start()
-        v_out[b].start()
         o3[b] = jnp.dot(weights.astype(BF16), vbuf[b].reshape(width, head_dim), preferred_element_type=F32)
         m3[b] = jnp.broadcast_to(top, (heads, 128))
         l3[b] = jnp.broadcast_to(jnp.sum(weights, axis=1, keepdims=True), (heads, 128))
@@ -145,9 +140,20 @@
         stats = jnp.where(lane == j, m3[:, j, :], stats)
         stats = jnp.where(lane == heads + j, l3[:, j, :], stats)
     packed_ref[:, q_width:q_width + 128] = stats
+
+
+def write_kernel(kbuf, vbuf, wo, new_k, new_v, wo_buf, ksem, vsem, wsem):
+    rows = kbuf.shape[0]
+    width = wo_buf.shape[1]
+    cols = pl.ds(pl.multiple_of(lax.axis_index("sp") * width, 128), width)
+    copies = [pltpu.make_async_copy(wo.at[:, cols], wo_buf, wsem)]
     for b in range(rows):
-        k_out[b].wait()
-        v_out[b].wait()
+        copies.append(pltpu.make_async_copy(kbuf.at[b], new_k.at[b], ksem.at[b]))
+        copies.append(pltpu.make_async_copy(vbuf.at[b], new_v.at[b], vsem.at[b]))
+    for copy in copies:
+        copy.start()
+    for copy in copies:
+        copy.wait()
 
 
 def exchange(axis, source, slots_ref, cols, send_sem, recv_sem):
@@ -175,12 +181,14 @@
     return total
 
 
-def mlp_kernel(head_dim, cuts, packed_ref, tokens, gain, wo, wg, wu, wd, out_ref,
-               tok_ref, gain_ref, wo_buf, wgu_buf, wd_buf, r1, part2, r2, part3, r3, part4, r4, part5, r5, part6, r6,
-               psem, wsem, gsem, dsem, ssem, rsem):
+def mlp_kernel(head_dim, cuts, sp_size, *refs):
+    r1 = refs[:sp_size]
+    (wo_buf, tokens, gain, wg, wu, wd, out_ref,
+               tok_ref, gain_ref, wgu_buf, wd_buf, part2, r2, part3, r3, part4, r4, part5, r5, part6, r6,
+               psem, gsem, dsem, ssem, rsem) = refs[sp_size:]
     rows, depth = tokens.shape
-    sp_size, tp_size = r1.shape[0], r2.shape[0]
-    q_width = wo.shape[0]
+    tp_size = r2.shape[0]
+    q_width = wo_buf.shape[0]
     heads = q_width // head_dim
     width = depth // sp_size
     sp = lax.axis_index("sp")
@@ -194,7 +202,6 @@
         for d in range(1, size):
             pl.semaphore_signal(barrier, inc=1, device_id={axis: lax.rem(me + d, size)}, device_id_type=MESH)
     small = [pltpu.make_async_copy(tokens.at[:, my_cols], tok_ref, psem.at[0]), pltpu.make_async_copy(gain, gain_ref, psem.at[1])]
-    o_load = pltpu.make_async_copy(wo.at[:, my_cols], wo_buf, wsem)
     gate_loads, down_loads = [], []
     for i, piece in enumerate(pieces):
         cols = pl.ds(start + piece.start, piece.size)
@@ -205,22 +212,15 @@
             pltpu.make_async_copy(wd.at[pl.ds(s * width + piece.start, piece.size), my_cols],
                                   wd_buf.at[pl.ds(sp_size * piece.start + s * piece.size, piece.size), :], dsem.at[i, s])
             for s in range(sp_size)])
-    o_load.start()
     for copy in small:
         copy.start()
     for loads in gate_loads:
         for copy in loads:
             copy.start()
-    pl.semaphore_wait(barrier, sp_size + tp_size - 2)
-
-    copies = exchange("sp", packed_ref, r1, pl.ds(0, packed_ref.shape[1]), ssem.at[0, 0], rsem.at[0, 0])
-    r1[sp] = packed_ref[...]
-    o_load.wait()
-    finish(copies)
     for loads in down_loads:
         for copy in loads:
             copy.start()
-    stats = [r1[s, :, q_width:q_width + 128] for s in range(sp_size)]
+    stats = [r1[s][:, q_width:q_width + 128] for s in range(sp_size)]
     parts = []
     for j in range(heads):
         tops = [t[:, j * 16:j * 16 + 1] for t in stats]
@@ -229,7 +229,7 @@
         denominator = jnp.zeros((rows, 1), F32)
         for s in range(sp_size):
             factor = jnp.exp(tops[s] - best)
-            numerator = numerator + r1[s, :, j * head_dim:(j + 1) * head_dim] * factor
+            numerator = numerator + r1[s][:, j * head_dim:(j + 1) * head_dim] * factor
             denominator = denominator + stats[s][:, (heads + j) * 16:(heads + j) * 16 + 1] * factor
         parts.append((numerator / denominator).astype(BF16))
     attended = jnp.concatenate(parts, axis=1)
@@ -238,6 +238,8 @@
         sent = []
         for i, piece in enumerate(pieces):
             source[:, piece] = sum(jnp.dot(l, w[:, piece], preferred_element_type=F32) for l, w in zip(left, weights))
+            if i == 0:
+                pl.semaphore_wait(barrier, sp_size + tp_size - 2)
             sent.append(exchange("tp", source, slots_ref, piece, ssem.at[phase, i], rsem.at[phase, i]))
             slots_ref[tp, :, piece] = source[:, piece]
         return sent
@@ -252,11 +254,11 @@
             target_slots[sp, :, piece] = value
         return passed
 
-    sent = project([attended], [wo_buf], part2, r2, 1)
+    sent = project([attended], [wo_buf], part2, r2, 0)
     finish(small)
     tok32 = tok_ref[...].astype(F32)
     part6[...] = tok32
-    passed = settle(part6, sent, r2, part3, r3, 2)
+    passed = settle(part6, sent, r2, part3, r3, 1)
     for loads in gate_loads:
         finish(loads)
     for copies in passed:
@@ -270,7 +272,7 @@
         gate, up = both[:, :piece.size], both[:, piece.size:]
         active = (gate * jax.nn.sigmoid(gate) * up).astype(BF16).astype(F32)
         part4[:, piece] = active
-        moved.append(exchange("sp", part4, r4, piece, ssem.at[3, i], rsem.at[3, i]))
+        moved.append(exchange("sp", part4, r4, piece, ssem.at[2, i], rsem.at[2, i]))
         r4[sp, :, piece] = active
     left, weights = [], []
     for i, piece in enumerate(pieces):
@@ -287,9 +289,9 @@
     sent = []
     for i, piece in enumerate(pieces):
         part5[:, piece] = part5[:, piece] + jnp.dot(left, rows_of[:, piece.start:piece.start + piece.size], preferred_element_type=F32)
-        sent.append(exchange("tp", part5, r5, piece, ssem.at[4, i], rsem.at[4, i]))
+        sent.append(exchange("tp", part5, r5, piece, ssem.at[3, i], rsem.at[3, i]))
         r5[tp, :, piece] = part5[:, piece]
-    passed = settle(part3, sent, r5, part6, r6, 5)
+    passed = settle(part3, sent, r5, part6, r6, 4)
     for copies in passed:
         finish(copies)
     out_ref[...] = jnp.concatenate([r6[s] for s in range(sp_size)], axis=1).astype(BF16)
@@ -317,50 +319,62 @@
         hbm = pl.BlockSpec(memory_space=pltpu.HBM)
         dma = pltpu.SemaphoreType.DMA
         in_hbm = functools.partial(pltpu.with_memory_space_constraint, memory_space=pltpu.HBM)
-        new_k, new_v, packed = pl.pallas_call(
+        k_here, v_here, packed = pl.pallas_call(
             functools.partial(attention_kernel, sp_size, chunks),
-            out_shape=[pltpu.HBM(cache_k.shape, BF16), pltpu.HBM(cache_v.shape, BF16),
+            out_shape=[pltpu.VMEM(cache_k.shape, BF16), pltpu.VMEM(cache_v.shape, BF16),
                        pltpu.VMEM((rows, q_width + 128), F32)],
             in_specs=[hbm] * 8,
-            out_specs=[hbm, hbm, vmem],
+            out_specs=[vmem] * 3,
             scratch_shapes=[
                 pltpu.SMEM((rows,), jnp.int32), pltpu.VMEM((rows, depth), BF16), pltpu.VMEM((depth // 128, 128), BF16),
                 pltpu.VMEM((depth, q_width + 2 * kv_width), BF16),
-                pltpu.VMEM(cache_k.shape, BF16), pltpu.VMEM(cache_v.shape, BF16),
                 pltpu.VMEM((rows, heads, head_dim), F32), pltpu.VMEM((rows, kv_local, head_dim), F32),
                 pltpu.VMEM((rows, kv_local, head_dim), F32), pltpu.VMEM((rows, heads, head_dim), F32),
                 pltpu.VMEM((rows, heads, 128), F32), pltpu.VMEM((rows, heads, 128), F32),
-                dma((3,)), dma((chunks, 3)), dma((rows,)), dma((rows,)), dma((rows,)), dma((rows,)),
+                dma((3,)), dma((chunks, 3)), dma((rows,)), dma((rows,)),
             ],
-            compiler_params=pltpu.CompilerParams(vmem_limit_bytes=40 * 2 ** 20),
+            compiler_params=pltpu.CompilerParams(vmem_limit_bytes=20 * 2 ** 20),
             cost_estimate=pl.CostEstimate(flops=10 ** 9, bytes_accessed=48 * 10 ** 6, transcendentals=0),
             name="attention",
         )(*map(in_hbm, (positions, tokens, attn_gain.reshape(depth // 128, 128), w_q, w_k, w_v, cache_k, cache_v)))
 
+        parts = [packed]
+        for d in range(1, sp_size):
+            parts.append(lax.ppermute(packed, "sp", [(i, (i + d) % sp_size) for i in range(sp_size)]))
+        in_vmem = functools.partial(pltpu.with_memory_space_constraint, memory_space=pltpu.VMEM)
+        new_k, new_v, wo_here = pl.pallas_call(
+            write_kernel,
+            out_shape=[pltpu.HBM(cache_k.shape, BF16), pltpu.HBM(cache_v.shape, BF16), pltpu.VMEM((q_width, width), BF16)],
+            in_specs=[vmem, vmem, hbm],
+            out_specs=[hbm, hbm, vmem],
+            scratch_shapes=[dma((rows,)), dma((rows,)), dma],
+            compiler_params=pltpu.CompilerParams(vmem_limit_bytes=4 * 2 ** 20),
+            cost_estimate=pl.CostEstimate(flops=5 * 10 ** 9, bytes_accessed=18 * 10 ** 6, transcendentals=0),
+            name="write",
+        )(in_vmem(k_here), in_vmem(v_here), in_hbm(w_o))
+
         chunk = pltpu.VMEM((rows, width), F32)
         act = pltpu.VMEM((rows, hidden_width), F32)
         out = pl.pallas_call(
-            functools.partial(mlp_kernel, head_dim, cuts),
+            functools.partial(mlp_kernel, head_dim, cuts, sp_size),
             out_shape=jax.ShapeDtypeStruct((rows, depth), BF16),
-            in_specs=[vmem] + [hbm] * 6,
+            in_specs=[vmem] * (sp_size + 1) + [hbm] * 5,
             out_specs=vmem,
             scratch_shapes=[
                 pltpu.VMEM((rows, width), BF16), pltpu.VMEM((depth // 128, 128), BF16),
-                pltpu.VMEM((q_width, width), BF16), pltpu.VMEM((depth, 2 * hidden_width), BF16),
-                pltpu.VMEM((w_down.shape[0], width), BF16),
-                pltpu.VMEM((sp_size, rows, q_width + 128), F32),
+                pltpu.VMEM((depth, 2 * hidden_width), BF16), pltpu.VMEM((w_down.shape[0], width), BF16),
                 chunk, pltpu.VMEM((tp_size, rows, width), F32),
                 chunk, pltpu.VMEM((sp_size, rows, width), F32),
                 act, pltpu.VMEM((sp_size, rows, hidden_width), F32),
                 chunk, pltpu.VMEM((tp_size, rows, width), F32),
                 chunk, pltpu.VMEM((sp_size, rows, width), F32),
-                dma((2,)), dma, dma((len(cuts), 2)), dma((len(cuts), sp_size)),
-                dma((6, len(cuts), 3)), dma((6, len(cuts), 3)),
+                dma((2,)), dma((len(cuts), 2)), dma((len(cuts), sp_size)),
+                dma((5, len(cuts), 3)), dma((5, len(cuts), 3)),
             ],
-            compiler_params=pltpu.CompilerParams(vmem_limit_bytes=40 * 2 ** 20, collective_id=0, has_side_effects=True),
+            compiler_params=pltpu.CompilerParams(vmem_limit_bytes=26 * 2 ** 20, collective_id=0, has_side_effects=True),
             cost_estimate=pl.CostEstimate(flops=10 ** 9, bytes_accessed=21 * 10 ** 6, transcendentals=0),
             name="mlp",
-        )(packed, *map(in_hbm, (tokens, mlp_gain.reshape(depth // 128, 128), w_o, w_gate, w_up, w_down)))
+        )(*map(in_vmem, parts + [wo_here]), *map(in_hbm, (tokens, mlp_gain.reshape(depth // 128, 128), w_gate, w_up, w_down)))
         return out, new_k, new_v
 
     return jax.shard_map(local_step, mesh=mesh, in_specs=in_specs, out_specs=out_specs, check_vma=False)

time: 47.9 us -> 51 us (1.065)
  starting transfers between devices: 0 us -> 4.52 us
  Pallas kernels: 46.5 us -> 45 us
    ppermute x0 -> x3, starting transfers between devices: none -> 4.52 us  [local_step(): lax.ppermute(packed, 'sp', [(i, (i + d) % sp_size) for i in range(sp_size)])]
    pallas_call x1, Pallas kernels: 17.1 us -> 15.5 us  [local_step(): pl.pallas_call(functools.partial(attention_kernel, sp_size, chunks), out_...]
    pallas_call x1 -> x2, Pallas kernels: 29.4 us -> 29.5 us  [the longest x1 23.5 us: local_step(): pl.pallas_call(functools.partial(mlp_kernel, head_dim, cuts, sp_size), ou...]
  transfers between devices with their start and end apart: 0 -> 3, of which waited for: 0 -> 0; matrix products, arithmetic and copies ran while one was open for 0% -> 0% of each run, Pallas kernels for 0% -> 12%
where the time goes in v3:
time: 51 us; the launch traced here: 50.8 us
  Pallas kernels  45 us (88%)
  starting transfers between devices  4.52 us (9%)
  between operations  0.68 us (1%)
  local copies, waits for them, and re-layouts  0.63 us (1%)
    pallas_call x1, Pallas kernels, local_step(): pl.pallas_call(functools.partial(mlp_kernel, head_dim, cuts, sp_size), ou...  23.5 us
    pallas_call x1, Pallas kernels, local_step(): pl.pallas_call(functools.partial(attention_kernel, sp_size, chunks), out_...  15.5 us
    pallas_call x1, Pallas kernels, local_step(): pl.pallas_call(write_kernel, out_shape=[pltpu.HBM(cache_k.shape, BF16), p...  6.01 us
    ppermute x3, starting transfers between devices, local_step(): lax.ppermute(packed, 'sp', [(i, (i + d) % sp_size) for i in range(sp_size)])  4.52 us
  transfers between devices with their start and end apart: 3, of which 0 were waited for; matrix products, arithmetic and copies ran while one was open for 0% of the time, Pallas kernels for 12%

profile of v3, /device:TPU:0, one launch (start us, length us, event | category | flops | bytes accessed | tf_op | source)
XLA Modules:
  0.0 50.8 jit_solution(13069211251962168403)
XLA Ops:
  0.6 15.5 %attention.1 = (bf16[8,1024,2,256]{3,2,1,0:T(2,128)(2,1)S(1)}, bf16[8,1024,2,256]{3,2,1,0:T(2,128)(2,1)S(1)}, f32[8,1152]{1,0:T(8,128)S(1)}) custom-call(s32[8]{0:T(128)} %positions.1, bf16[8,3584]{1,0:T(8,128)(2,1)} %refs_5_.1, bf16[28,128]{1,0:T(8,128)(2,1)} %bitcast.2, bf16[3584,1024]{1,0:T(8,128)(2,1)} %wq.1, bf16[3584,512]{1,0:T(8,128)(2,1)} %wk.1, ...), custom_call_target="tpu_custom_call" | custom-call | flops 1000000000 | bytes 48000000 | tf_op jit(solution)/shard_map/attention/pallas_call | solution.py:322
  16.1 0.5 %collective-permute-start = (f32[8,1152]{1,0:T(8,128)S(1)}, f32[8,1152]{1,0:T(8,128)S(1)}, u32[]{:S(2)}, u32[]{:S(2)}) collective-permute-start(f32[8,1152]{1,0:T(8,128)S(1)} %get-tuple-element.9.refs_0_), channel_id=1, source_target_pairs={{0,1},{1,2},{2,3},{3,0},{4,5},{5,6},{6,7},{7,4},{8,9},{9,10},{10,1... | collective-permute-start | bytes 110600 | tf_op jit(solution)/shard_map/ppermute | solution.py:343
  16.7 2.6 %collective-permute-start.1 = (f32[8,1152]{1,0:T(8,128)S(1)}, f32[8,1152]{1,0:T(8,128)S(1)}, u32[]{:S(2)}, u32[]{:S(2)}) collective-permute-start(f32[8,1152]{1,0:T(8,128)S(1)} %get-tuple-element.9.refs_0_), channel_id=1, source_target_pairs={{0,2},{1,3},{2,0},{3,1},{4,6},{5,7},{6,4},{7,5},{8,10},{9,11},{10,... | collective-permute-start | bytes 110600 | tf_op jit(solution)/shard_map/ppermute | solution.py:343
  19.3 1.4 %collective-permute-start.2 = (f32[8,1152]{1,0:T(8,128)S(1)}, f32[8,1152]{1,0:T(8,128)S(1)}, u32[]{:S(2)}, u32[]{:S(2)}) collective-permute-start(f32[8,1152]{1,0:T(8,128)S(1)} %get-tuple-element.9.refs_0_), channel_id=1, source_target_pairs={{0,3},{1,0},{2,1},{3,2},{4,7},{5,4},{6,5},{7,6},{8,11},{9,8},{10,9... | collective-permute-start | bytes 110600 | tf_op jit(solution)/shard_map/ppermute | solution.py:343
  20.7 6.0 %write.1 = (bf16[8,1024,2,256]{3,2,1,0:T(2,128)(2,1)}, bf16[8,1024,2,256]{3,2,1,0:T(2,128)(2,1)}, bf16[1024,896]{1,0:T(8,128)(2,1)S(1)}) custom-call(bf16[8,1024,2,256]{3,2,1,0:T(2,128)(2,1)S(1)} %get-tuple-element.10.kbuf, bf16[8,1024,2,256]{3,2,1,0:T(2,128)(2,1)S(1)} %get-tuple-element.11.vbuf, bf16[1024,3584]{1,0:T(8,128)(2,1)} %wo.1), custom_call_target="tpu_custom_call" | custom-call | flops 5000000000 | bytes 18000000 | tf_op jit(solution)/shard_map/write/pallas_call | solution.py:345
  26.7 0.0 collective-permute-done.refs_1_
  26.7 0.0 collective-permute-done.1.refs_2_
  26.7 0.0 collective-permute-done.2.refs_3_
  26.7 23.5 %mlp.1 = bf16[8,3584]{1,0:T(8,128)(2,1)S(1)} custom-call(f32[8,1152]{1,0:T(8,128)S(1)} %get-tuple-element.9.refs_0_, f32[8,1152]{1,0:T(8,128)S(1)} %collective-permute-done.refs_1_, f32[8,1152]{1,0:T(8,128)S(1)} %collective-permute-done.1.refs_2_, f32[8,1152]{1,0:T(8,128)S(1)} %collective-permute-done.2.refs_3_, ...), custom_call_target="tpu_custom_call" | custom-call | flops 1000000000 | bytes 21000000 | tf_op jit(solution)/shard_map/mlp/pallas_call | solution.py:358
  50.2 0.6 %copy.17 = bf16[8,3584]{1,0:T(8,128)(2,1)} copy(bf16[8,3584]{1,0:T(8,128)(2,1)S(1)} %mlp.1) | data formatting | bytes 114688
Async XLA Ops:
  16.1 10.5 %collective-permute-start = (f32[8,1152]{1,0:T(8,128)S(1)}, f32[8,1152]{1,0:T(8,128)S(1)}, u32[]{:S(2)}, u32[]{:S(2)}) collective-permute-start(f32[8,1152]{1,0:T(8,128)S(1)} %get-tuple-element.9.refs_0_), channel_id=1, source_target_pairs={{0,1},{1,2},{2,3},{3,0},{4,5},{5,6},{6,7},{7,4},{8,9},{9,10},{10,1... | collective-permute-start | bytes 110600 | tf_op jit(solution)/shard_map/ppermute | solution.py:343
  16.7 10.0 %collective-permute-start.1 = (f32[8,1152]{1,0:T(8,128)S(1)}, f32[8,1152]{1,0:T(8,128)S(1)}, u32[]{:S(2)}, u32[]{:S(2)}) collective-permute-start(f32[8,1152]{1,0:T(8,128)S(1)} %get-tuple-element.9.refs_0_), channel_id=1, source_target_pairs={{0,2},{1,3},{2,0},{3,1},{4,6},{5,7},{6,4},{7,5},{8,10},{9,11},{10,... | collective-permute-start | bytes 110600 | tf_op jit(solution)/shard_map/ppermute | solution.py:343
  19.3 7.4 %collective-permute-start.2 = (f32[8,1152]{1,0:T(8,128)S(1)}, f32[8,1152]{1,0:T(8,128)S(1)}, u32[]{:S(2)}, u32[]{:S(2)}) collective-permute-start(f32[8,1152]{1,0:T(8,128)S(1)} %get-tuple-element.9.refs_0_), channel_id=1, source_target_pairs={{0,3},{1,0},{2,1},{3,2},{4,7},{5,4},{6,5},{7,6},{8,11},{9,8},{10,9... | collective-permute-start | bytes 110600 | tf_op jit(solution)/shard_map/ppermute | solution.py:343

commit v4 on v0

v4 whole, which is shorter than its diff:
```python
import math
import functools
import jax
import jax.numpy as jnp
from jax import lax
from jax.experimental import pallas as pl
from jax.experimental.pallas import tpu as pltpu
from jax.sharding import PartitionSpec as P

NORM_EPS = 1e-5
ROPE_THETA = 10000.0
MESH = pl.DeviceIdType.MESH
F32 = jnp.float32
BF16 = jnp.bfloat16


def rope_tables(positions, half):
    index = lax.broadcasted_iota(jnp.int32, (positions.shape[0], half), 1).astype(F32)
    angles = positions * jnp.exp(index * (-math.log(ROPE_THETA) / half))
    turns = jnp.floor(angles * (2.0 / math.pi) + 0.5)
    rest = ((angles - turns * 1.5703125) - turns * 4.837512969970703125e-4) - turns * 7.54978995489188216e-8
    square = rest * rest
    sine = rest + rest * square * (-1.0 / 6 + square * (1.0 / 120 + square * (-1.0 / 5040 + square * (1.0 / 362880))))
    cosine = 1.0 + square * (-0.5 + square * (1.0 / 24 + square * (-1.0 / 720 + square * (1.0 / 40320 - square * (1.0 / 3628800)))))
    quadrant = turns.astype(jnp.int32) & 3
    swap = (quadrant & 1) == 1
    cos_value = jnp.where(swap, sine, cosine)
    sin_value = jnp.where(swap, cosine, sine)
    return (jnp.where((quadrant == 1) | (quadrant == 2), -cos_value, cos_value),
            jnp.where(quadrant >= 2, -sin_value, sin_value))


def scaled_norm(wide, gain_ref):
    inv_rms = lax.rsqrt(jnp.mean(wide * wide, axis=-1, keepdims=True) + NORM_EPS)
    gain = gain_ref[...].astype(F32)
    pieces = [(wide[:, i * 128:(i + 1) * 128] * inv_rms * gain[i:i + 1]).astype(BF16) for i in range(wide.shape[1] // 128)]
    return jnp.concatenate(pieces, axis=1)


def exchange(axis, source, slots_ref, send_sem, recv_sem):
    me = lax.axis_index(axis)
    size = slots_ref[0].shape[0]
    dst, cols = slots_ref
    copies = []
    for i in range(size - 1):
        down, up = size - 1 - i, i
        low = jnp.where(down > me, down, down - 1)
        high = jnp.where(up < me, up, up + 1)
        peer = jnp.where(me < size // 2, low, high)
        copies.append((
            pltpu.make_async_remote_copy(
                src_ref=source, dst_ref=dst.at[(me,) + cols], send_sem=send_sem.at[peer], recv_sem=recv_sem.at[me],
                device_id={axis: peer}, device_id_type=MESH),
            pltpu.make_async_remote_copy(
                src_ref=source, dst_ref=dst.at[(peer,) + cols], send_sem=send_sem.at[peer], recv_sem=recv_sem.at[peer],
                device_id={axis: peer}, device_id_type=MESH)))
        copies[-1][0].start()
    return copies


def finish(copies):
    for sent, arriving in copies:
        arriving.wait_recv()
    for sent, arriving in copies:
        sent.wait_send()


def added(slots_ref, cols):
    total = slots_ref[0, :, cols]
    for t in range(1, slots_ref.shape[0]):
        total = total + slots_ref[t, :, cols]
    return total


def layer_kernel(sp_size, tp_size, cuts, positions, tokens, attn_gain, mlp_gain, wq, wk, wv, ck, cv, wo, wg, wu, wd,
                 kbuf, vbuf, k_row, v_row, out_ref,
                 pos_ref, tok_ref, tok_cols, ag_ref, mg_ref, wqkv_buf, wo_buf, wgu_buf, wd_buf,
                 part0, r0, q3, k3, v3, o3, m3, l3, part1, r1, att, part2, r2, part3, r3, part4, r4, part5, r5, part6, r6,
                 psem, wsem, ksem, vsem, osem, gsem, dsem, ssem0, rsem0, ssem1, rsem1, ssem, rsem):
    rows, depth = tokens.shape
    _, local_slots, kv_local, head_dim = ck.shape
    slots = local_slots * sp_size
    q_width, kv_width = wq.shape[1], wk.shape[1]
    heads = q_width // head_dim
    group = heads // kv_local
    half = head_dim // 2
    width = depth // sp_size
    q_cols, kv_cols = q_width // sp_size, kv_width // sp_size
    flat = local_slots * kv_local
    sp, tp = lax.axis_index("sp"), lax.axis_index("tp")
    first_slot = sp * local_slots
    start = pl.multiple_of(sp * width, 128)
    my_cols = pl.ds(start, width)
    pieces = [pl.ds(a, b - a) for a, b in zip((0,) + cuts[:-1], cuts)]

    barrier = pltpu.get_barrier_semaphore()
    for axis, me, size in (("sp", sp, sp_size), ("tp", tp, tp_size)):
        for d in range(1, size):
            pl.semaphore_signal(barrier, inc=1, device_id={axis: lax.rem(me + d, size)}, device_id_type=MESH)

    small = [pltpu.make_async_copy(tokens, tok_ref, psem.at[0]), pltpu.make_async_copy(attn_gain, ag_ref, psem.at[1]),
             pltpu.make_async_copy(positions, pos_ref, psem.at[2]), pltpu.make_async_copy(mlp_gain, mg_ref, psem.at[3]),
             pltpu.make_async_copy(tokens.at[:, my_cols], tok_cols, psem.at[4])]
    q_part = pl.ds(pl.multiple_of(sp * q_cols, 128), q_cols)
    kv_part = pl.ds(pl.multiple_of(sp * kv_cols, 128), kv_cols)
    qkv_loads = [pltpu.make_async_copy(wq.at[:, q_part], wqkv_buf.at[:, pl.ds(0, q_cols)], wsem.at[0]),
                 pltpu.make_async_copy(wk.at[:, kv_part], wqkv_buf.at[:, pl.ds(q_cols, kv_cols)], wsem.at[1]),
                 pltpu.make_async_copy(wv.at[:, kv_part], wqkv_buf.at[:, pl.ds(q_cols + kv_cols, kv_cols)], wsem.at[2])]
    k_flat, v_flat = ck.reshape(rows, flat, head_dim), cv.reshape(rows, flat, head_dim)
    k_in = [pltpu.make_async_copy(k_flat.at[b], kbuf.at[b], ksem.at[b]) for b in range(rows)]
    v_in = [pltpu.make_async_copy(v_flat.at[b], vbuf.at[b], vsem.at[b]) for b in range(rows)]
    o_load = pltpu.make_async_copy(wo.at[:, my_cols], wo_buf, osem)
    gate_loads, down_loads = [], []
    for i, piece in enumerate(pieces):
        cols = pl.ds(start + piece.start, piece.size)
        gate_loads.append([
            pltpu.make_async_copy(wg.at[:, cols], wgu_buf.at[:, pl.ds(2 * piece.start, piece.size)], gsem.at[i, 0]),
            pltpu.make_async_copy(wu.at[:, cols], wgu_buf.at[:, pl.ds(2 * piece.start + piece.size, piece.size)], gsem.at[i, 1])])
        down_loads.append([
            pltpu.make_async_copy(wd.at[pl.ds(s * width + piece.start, piece.size), my_cols],
                                  wd_buf.at[pl.ds(sp_size * piece.start + s * piece.size, piece.size), :], dsem.at[i, s])
            for s in range(sp_size)])
    for copy in small + qkv_loads:
        copy.start()
    for b in range(rows):
        k_in[b].start()
        v_in[b].start()
    o_load.start()
    for loads in gate_loads + down_loads:
        for copy in loads:
            copy.start()

    for copy in small:
        copy.wait()
    normed = scaled_norm(tok_ref[...].astype(F32), ag_ref)
    for copy in qkv_loads:
        copy.wait()
    mine = jnp.dot(normed, wqkv_buf[...], preferred_element_type=F32)
    part0[...] = mine
    pl.semaphore_wait(barrier, sp_size + tp_size - 2)
    moved = exchange("sp", part0, (r0, ()), ssem0, rsem0)
    r0[sp] = mine

    row = lax.broadcasted_iota(jnp.int32, (rows, half), 0)
    position_rows = jnp.zeros((rows, half), F32)
    for b in range(rows):
        position_rows = jnp.where(row == b, pos_ref[b].astype(F32), position_rows)
    cos_table, sin_table = rope_tables(position_rows, half)
    scale = 1.0 / math.sqrt(head_dim)
    column = lax.broadcasted_iota(jnp.int32, (heads, flat), 1)
    own_head = lax.rem(column, kv_local) == lax.broadcasted_iota(jnp.int32, (heads, flat), 0) // group
    slot_ids = first_slot + column // kv_local
    finish(moved)

    def rotate(a, b):
        return a * cos_table - b * sin_table, b * cos_table + a * sin_table

    def gathered(offset, size, index):
        s, at = index * half // size, index * half % size
        return r0[s, :, offset + at:offset + at + half]

    for j in range(heads):
        a, b = rotate(gathered(0, q_cols, 2 * j), gathered(0, q_cols, 2 * j + 1))
        q3[:, j, 0:half] = a
        q3[:, j, half:head_dim] = b
    for j in range(kv_local):
        a, b = rotate(gathered(q_cols, kv_cols, 2 * j), gathered(q_cols, kv_cols, 2 * j + 1))
        k3[:, j, 0:half] = a
        k3[:, j, half:head_dim] = b
        v3[:, j, 0:half] = gathered(q_cols + kv_cols, kv_cols, 2 * j)
        v3[:, j, half:head_dim] = gathered(q_cols + kv_cols, kv_cols, 2 * j + 1)
    k_row[...] = k3[...].astype(BF16)
    v_row[...] = v3[...].astype(BF16)

    def per_query(pair):
        return jnp.concatenate([jnp.broadcast_to(pair[h:h + 1], (group, head_dim)) for h in range(kv_local)], axis=0)

    sends = []
    side = part1.shape[1]
    lane = lax.broadcasted_iota(jnp.int32, (side, 128), 1) // 16
    for b in range(rows):
        position = pos_ref[b]
        target = lax.rem(position, slots)
        limit = jnp.where(position >= slots - 1, slots, position)
        k_in[b].wait()
        v_in[b].wait()
        q_b = q3[b].astype(BF16)
        new_key = per_query(k3[b].astype(BF16).astype(F32))
        new_value = per_query(v3[b].astype(BF16).astype(F32))
        new_score = jnp.sum(q_b.astype(F32) * new_key, axis=1, keepdims=True) * scale
        scores = lax.dot_general(q_b, kbuf[b], (((1,), (1,)), ((), ())), preferred_element_type=F32) * scale
        fresh = slot_ids == target
        valid = own_head & (slot_ids <= limit)
        scores = jnp.where(valid, jnp.where(fresh, new_score, scores), -jnp.inf)
        top = jnp.max(scores, axis=1, keepdims=True)
        weights = jnp.where(valid, jnp.exp(scores - top), 0.0)
        stored = jnp.where(fresh, 0.0, weights)
        new_weight = jnp.sum(jnp.where(fresh, weights, 0.0), axis=1, keepdims=True)
        o3[b] = (jnp.dot(stored.astype(BF16), vbuf[b], preferred_element_type=F32)
                 + new_weight.astype(BF16).astype(F32) * new_value)
        m3[b] = jnp.broadcast_to(top, (heads, 128))
        l3[b] = jnp.broadcast_to(jnp.sum(weights, axis=1, keepdims=True), (heads, 128))
        if (b + 1) % side == 0:
            g = b // side
            members = pl.ds(g * side, side)
            stats = jnp.zeros((side, 128), F32)
            for j in range(heads):
                part1[g, :, j * head_dim:(j + 1) * head_dim] = o3[members, j, :]
                stats = jnp.where(lane == j, m3[members, j, :], stats)
                stats = jnp.where(lane == heads + j, l3[members, j, :], stats)
            part1[g, :, q_width:q_width + 128] = stats
            sends.append(exchange("sp", part1.at[g], (r1, (g,)), ssem1.at[g], rsem1.at[g]))
            r1[sp, g] = part1[g]

    for g, copies in enumerate(sends):
        finish(copies)
        stats = [r1[s, g, :, q_width:q_width + 128] for s in range(sp_size)]
        for j in range(heads):
            tops = [t[:, j * 16:j * 16 + 1] for t in stats]
            best = functools.reduce(jnp.maximum, tops)
            numerator = jnp.zeros((side, head_dim), F32)
            denominator = jnp.zeros((side, 1), F32)
            for s in range(sp_size):
                factor = jnp.exp(tops[s] - best)
                numerator = numerator + r1[s, g, :, j * head_dim:(j + 1) * head_dim] * factor
                denominator = denominator + stats[s][:, (heads + j) * 16:(heads + j) * 16 + 1] * factor
            att[g * side:(g + 1) * side, j * head_dim:(j + 1) * head_dim] = numerator / denominator
    attended = att[...].astype(BF16)

    def pass_on(axis, me, source, slots_ref, phase, i):
        piece = pieces[i]
        copies = exchange(axis, source.at[:, piece], (slots_ref, (slice(None), piece)), ssem.at[phase, i], rsem.at[phase, i])
        slots_ref[me, :, piece] = source[:, piece]
        return copies

    def settle(base, sent, slots_ref, target, target_slots, phase):
        passed = []
        for i, piece in enumerate(pieces):
            finish(sent[i])
            target[:, piece] = (base[:, piece] + added(slots_ref, piece)).astype(BF16).astype(F32)
            passed.append(pass_on("sp", sp, target, target_slots, phase, i))
        return passed

    o_load.wait()
    sent = []
    for i, piece in enumerate(pieces):
        part2[:, piece] = jnp.dot(attended, wo_buf[:, piece], preferred_element_type=F32)
        sent.append(pass_on("tp", tp, part2, r2, 0, i))
    part6[...] = tok_cols[...].astype(F32)
    passed = settle(part6, sent, r2, part3, r3, 1)
    for loads in gate_loads + down_loads:
        for copy in loads:
            copy.wait()
    for copies in passed:
        finish(copies)
    normed = scaled_norm(jnp.concatenate([r3[s] for s in range(sp_size)], axis=1), mg_ref)

    moved = []
    for i, piece in enumerate(pieces):
        both = jnp.dot(normed, wgu_buf[:, 2 * piece.start:2 * (piece.start + piece.size)], preferred_element_type=F32)
        gate, up = both[:, :piece.size], both[:, piece.size:]
        part4[:, piece] = (gate * jax.nn.sigmoid(gate) * up).astype(BF16).astype(F32)
        moved.append(pass_on("sp", sp, part4, r4, 2, i))
    total = None
    for i, piece in enumerate(pieces):
        finish(moved[i])
        left = jnp.concatenate([r4[s, :, piece] for s in range(sp_size)], axis=1).astype(BF16)
        down = pl.ds(sp_size * piece.start, sp_size * piece.size)
        if i + 1 < len(pieces):
            product = jnp.dot(left, wd_buf[down, :], preferred_element_type=F32)
            total = product if total is None else total + product
    part5[...] = total
    sent = []
    for i, piece in enumerate(pieces):
        part5[:, piece] = part5[:, piece] + jnp.dot(left, wd_buf[down, piece], preferred_element_type=F32)
        sent.append(pass_on("tp", tp, part5, r5, 3, i))
    passed = settle(part3, sent, r5, part6, r6, 4)
    for copies in passed:
        finish(copies)
    out_ref[...] = jnp.concatenate([r6[s] for s in range(sp_size)], axis=1).astype(BF16)


def write_kernel(sp_size, pos_ref, k_in, v_in, k_row, v_row, out_in, new_k, new_v, out_ref, kbuf, vbuf, ksem, vsem, osem):
    rows, local_slots, kv_local, head_dim = new_k.shape
    flat = local_slots * kv_local
    tile = 16
    first_slot = lax.axis_index("sp") * local_slots
    copies = [pltpu.make_async_copy(out_in, out_ref, osem)]
    k_flat, v_flat = new_k.reshape(rows, flat, head_dim), new_v.reshape(rows, flat, head_dim)
    for b in range(rows):
        target = lax.rem(pos_ref[b], local_slots * sp_size) - first_slot

        @pl.when((target >= 0) & (target < local_slots))
        def _():
            base = pl.multiple_of((target * kv_local) // tile * tile, tile)
            at = target * kv_local - base
            row = lax.broadcasted_iota(jnp.int32, (tile, head_dim), 0)
            for buf, fresh in ((kbuf, k_row), (vbuf, v_row)):
                block = buf[b, pl.ds(base, tile), :].astype(F32)
                pair = fresh[b].astype(F32)
                for h in range(kv_local):
                    block = jnp.where(row == at + h, pair[h:h + 1], block)
                buf[b, pl.ds(base, tile), :] = block.astype(BF16)

    for b in range(rows):
        copies.append(pltpu.make_async_copy(kbuf.at[b], k_flat.at[b], ksem.at[b]))
        copies.append(pltpu.make_async_copy(vbuf.at[b], v_flat.at[b], vsem.at[b]))
    for copy in copies:
        copy.start()
    for copy in copies:
        copy.wait()


def solution(mesh):
    sp_size, tp_size = mesh.shape["sp"], mesh.shape["tp"]
    cache_spec = P("dp", "sp", "tp", None)
    row_spec = P("dp", None)
    col_spec = P(None, "tp")
    in_specs = (row_spec, P("dp"), cache_spec, cache_spec, P(None), col_spec, col_spec, col_spec, P("tp", None), P(None), col_spec, col_spec, P("tp", None))
    out_specs = (row_spec, cache_spec, cache_spec)

    def local_step(tokens, positions, cache_k, cache_v, attn_gain, w_q, w_k, w_v, w_o, mlp_gain, w_gate, w_up, w_down):
        rows, depth = tokens.shape
        _, local_slots, kv_local, head_dim = cache_k.shape
        q_width, kv_width = w_q.shape[1], w_k.shape[1]
        heads = q_width // head_dim
        width = depth // sp_size
        cuts = (512, width)
        groups = 2
        flat_shape = (rows, local_slots * kv_local, head_dim)
        vmem = pl.BlockSpec(memory_space=pltpu.VMEM)
        hbm = pl.BlockSpec(memory_space=pltpu.HBM)
        dma = pltpu.SemaphoreType.DMA
        in_hbm = functools.partial(pltpu.with_memory_space_constraint, memory_space=pltpu.HBM)
        in_vmem = functools.partial(pltpu.with_memory_space_constraint, memory_space=pltpu.VMEM)
        f32 = lambda *shape: pltpu.VMEM(shape, F32)
        bf16 = lambda *shape: pltpu.VMEM(shape, BF16)
        qkv_cols = (q_width + 2 * kv_width) // sp_size
        packed = (groups, rows // groups, q_width + 128)
        k_here, v_here, k_row, v_row, out_here = pl.pallas_call(
            functools.partial(layer_kernel, sp_size, tp_size, cuts),
            out_shape=[bf16(*flat_shape), bf16(*flat_shape), bf16(rows, kv_local, head_dim), bf16(rows, kv_local, head_dim), bf16(rows, depth)],
            in_specs=[hbm] * 13,
            out_specs=[vmem] * 5,
            scratch_shapes=[
                pltpu.SMEM((rows,), jnp.int32), bf16(rows, depth), bf16(rows, width), bf16(depth // 128, 128), bf16(depth // 128, 128),
                bf16(depth, qkv_cols), bf16(q_width, width), bf16(depth, 2 * width), bf16(w_down.shape[0], width),
                f32(rows, qkv_cols), f32(sp_size, rows, qkv_cols),
                f32(rows, heads, head_dim), f32(rows, kv_local, head_dim), f32(rows, kv_local, head_dim),
                f32(rows, heads, head_dim), f32(rows, heads, 128), f32(rows, heads, 128),
                f32(*packed), f32(sp_size, *packed), f32(rows, q_width),
                f32(rows, width), f32(tp_size, rows, width), f32(rows, width), f32(sp_size, rows, width),
                f32(rows, width), f32(sp_size, rows, width), f32(rows, width), f32(tp_size, rows, width),
                f32(rows, width), f32(sp_size, rows, width),
                dma((5,)), dma((3,)), dma((rows,)), dma((rows,)), dma, dma((len(cuts), 2)), dma((len(cuts), sp_size)),
                dma((sp_size,)), dma((sp_size,)), dma((groups, sp_size)), dma((groups, sp_size)),
                dma((5, len(cuts), sp_size)), dma((5, len(cuts), sp_size)),
            ],
            compiler_params=pltpu.CompilerParams(vmem_limit_bytes=46 * 2 ** 20, collective_id=0, has_side_effects=True),
            cost_estimate=pl.CostEstimate(flops=10 ** 9, bytes_accessed=42 * 10 ** 6, transcendentals=0),
            name="layer",
        )(*map(in_hbm, (positions, tokens, attn_gain.reshape(depth // 128, 128), mlp_gain.reshape(depth // 128, 128),
                        w_q, w_k, w_v, cache_k, cache_v, w_o, w_gate, w_up, w_down)))

        new_k, new_v, out, _, _ = pl.pallas_call(
            functools.partial(write_kernel, sp_size),
            out_shape=[pltpu.HBM(cache_k.shape, BF16), pltpu.HBM(cache_v.shape, BF16), pltpu.HBM((rows, depth), BF16),
                       bf16(*flat_shape), bf16(*flat_shape)],
            in_specs=[pl.BlockSpec(memory_space=pltpu.SMEM)] + [vmem] * 5,
            out_specs=[hbm] * 3 + [vmem] * 2,
            scratch_shapes=[dma((rows,)), dma((rows,)), dma],
            input_output_aliases={1: 3, 2: 4},
            compiler_params=pltpu.CompilerParams(vmem_limit_bytes=4 * 2 ** 20),
            cost_estimate=pl.CostEstimate(flops=10 ** 9, bytes_accessed=17 * 10 ** 6, transcendentals=0),
            name="write",
        )(positions, *map(in_vmem, (k_here, v_here, k_row, v_row, out_here)))
        return out, new_k, new_v

    return jax.shard_map(local_step, mesh=mesh, in_specs=in_specs, out_specs=out_specs, check_vma=False)
```

time: 194 us -> 48.1 us (0.25)
  waiting for transfers between devices: 69.5 us -> 0 us
  matrix products: 51.9 us -> 0 us
  Pallas kernels: 0 us -> 47.3 us
  other arithmetic: 35 us -> 0 us
  blocking collectives: 19.1 us -> 0 us
  between operations: 14.2 us -> 0.66 us
  local copies, waits for them, and re-layouts: 3.89 us -> 0.01 us
    psum x2 -> x0, waiting for transfers between devices: 69.5 us -> none  [the longest x1 34.9 us: local_step(): lax.psum(jnp.dot(attended, w_o, preferred_element_type=jnp.float32), 'tp')]
    dot_general x8 -> x0, matrix products: 51.9 us -> none  [the longest x1 20.1 us: local_step(): jnp.dot(activated, w_down, preferred_element_type=jnp.float32)]
    pallas_call x0 -> x2, Pallas kernels: none -> 47.3 us  [the longest x1 40.6 us: local_step(): pl.pallas_call(functools.partial(layer_kernel, sp_size, tp_size, cuts), o...]
    select_n x1 -> x0, other arithmetic: 28.5 us -> none  [local_step(): new_v = jnp.where(hit_mask, v_new[:, None], cache_v)]
    psum x1 -> x0, blocking collectives: 10.6 us -> none  [local_step(): total = lax.psum(packed, 'sp')]
    pmax x1 -> x0, blocking collectives: 8.57 us -> none  [local_step(): global_max = lax.pmax(local_max, 'sp')]
    unnamed x12 -> x2, local copies, waits for them, and re-layouts: 3.42 us -> 0.01 us
    convert_element_type x5 -> x0, other arithmetic: 3.22 us -> none  [the longest x1 1.53 us: local_step(): layer_out = (hidden.astype(jnp.float32) + mlp_down).astype(jnp.bfloat16)]
  transfers between devices with their start and end apart: 2 -> 0, of which waited for: 2 -> 0; matrix products, arithmetic and copies ran while one was open for 0% -> 0% of each run, Pallas kernels for 0% -> 0%
where the time goes in v4:
time: 48.1 us; the launch traced here: 47.9 us
  Pallas kernels  47.3 us (98%)
  between operations  0.66 us (1%)
    pallas_call x1, Pallas kernels, local_step(): pl.pallas_call(functools.partial(layer_kernel, sp_size, tp_size, cuts), o...  40.6 us
    pallas_call x1, Pallas kernels, local_step(): pl.pallas_call(functools.partial(write_kernel, sp_size), out_shape=[pltpu...  6.67 us

profile of v4, /device:TPU:0, one launch (start us, length us, event | category | flops | bytes accessed | tf_op | source)
XLA Modules:
  0.0 47.9 jit_solution(15460595491477328682)
XLA Ops:
  0.6 0.0 copy-start
  0.6 40.6 %layer.1 = (bf16[8,2048,256]{2,1,0:T(8,128)(2,1)S(1)}, bf16[8,2048,256]{2,1,0:T(8,128)(2,1)S(1)}, bf16[8,2,256]{2,1,0:T(2,128)(2,1)S(1)}, bf16[8,2,256]{2,1,0:T(2,128)(2,1)S(1)}, bf16[8,3584]{1,0:T(8,128)(2,1)S(1)}) custom-call(s32[8]{0:T(128)} %pos_ref.1, bf16[8,3584]{1,0:T(8,128)(2,1)} %tokens.1, bf16[28,128]{1,0:T(8,128)(2,1)} %bitcast.2, ...), custom_call_target="tpu_custom_call" | custom-call | flops 1000000000 | bytes 42000000 | tf_op jit(solution)/shard_map/layer/pallas_call | solution.py:340
  41.2 0.0 copy-done
  41.3 6.7 %write.1 = (bf16[8,1024,2,256]{3,2,1,0:T(2,128)(2,1)}, bf16[8,1024,2,256]{3,2,1,0:T(2,128)(2,1)}, bf16[8,3584]{1,0:T(8,128)(2,1)}, bf16[8,2048,256]{2,1,0:T(8,128)(2,1)S(1)}, bf16[8,2048,256]{2,1,0:T(8,128)(2,1)S(1)}) custom-call(s32[8]{0:T(128)S(1)} %copy-done, ...), custom_call_target="tpu_custom_call", output_to_operand_aliasing={{3}: (1, {}), {4}: (2, {})} | custom-call | flops 1000000000 | bytes 17000000 | tf_op jit(solution)/shard_map/write/pallas_call | solution.py:365
Async XLA Ops:
  0.6 40.6 %copy-start = (s32[8]{0:T(128)S(1)}, s32[8]{0:T(128)}, u32[]{:S(2)}) copy-start(s32[8]{0:T(128)} %pos_ref.1) | copy-start | bytes 100
